TPU v7x, 32 devices: a whole 2x2x4 slice. The times are simulated.
32 devices in a mesh: gx: 4 (over x, core), gy: 8 (over z, y).
Axes of the slice: x: 2, y: 2, z: 4, core: 2. Of those that a mesh axis runs over, the one named last changes fastest.
Arguments:
- text_in: bfloat16 [32, 128, 768], P(('gx', 'gy')), may hold values from -6 to 6
- image_in: bfloat16 [32, 36, 1024], P(('gx', 'gy')), may hold values from -6 to 6
- text_lengths: int32 [32], P(('gx', 'gy')), may hold values from 8 to 128, as said below
- region_mask: int32 [32, 36], P(('gx', 'gy')), may hold values 0 or 1
- text_cot: bfloat16 [32, 128, 768], P(('gx', 'gy')), may hold values from -6 to 6
- image_cot: bfloat16 [32, 36, 1024], P(('gx', 'gy')), may hold values from -6 to 6
- co_text_proj: bfloat16 [3, 768, 1024], P(None, ('gx', 'gy')), may hold values from -0.21875 to 0.21875
- co_image_proj: bfloat16 [3, 1024, 1024], P(None, ('gx', 'gy')), may hold values from -0.1875 to 0.1875
- co_bias: bfloat16 [4, 1024], P(None, ('gx', 'gy')), may hold values from -3 to 3
- co_text_out: bfloat16 [1024, 768], P(('gx', 'gy')), may hold values from -0.75 to 0.75
- co_image_out: bfloat16 [1024, 1024], P(('gx', 'gy')), may hold values from -0.75 to 0.75
- text_up: bfloat16 [768, 3072], P(('gx', 'gy')), may hold values from -0.21875 to 0.21875
- text_up_bias: bfloat16 [3072], P(('gx', 'gy')), may hold values from -3 to 3
- text_down: bfloat16 [3072, 768], P(('gx', 'gy')), may hold values from -0.109375 to 0.109375
- image_up: bfloat16 [1024, 1024], P(('gx', 'gy')), may hold values from -0.1875 to 0.1875
- image_up_bias: bfloat16 [1024], P(('gx', 'gy')), may hold values from -3 to 3
- image_down: bfloat16 [1024, 1024], P(('gx', 'gy')), may hold values from -0.1875 to 0.1875
- text_self_qkv: bfloat16 [3, 768, 768], P(None, ('gx', 'gy')), may hold values from -0.21875 to 0.21875
- text_self_out: bfloat16 [768, 768], P(('gx', 'gy')), may hold values from -0.875 to 0.875
- image_self_qkv: bfloat16 [3, 1024, 1024], P(None, ('gx', 'gy')), may hold values from -0.1875 to 0.1875
- image_self_out: bfloat16 [1024, 1024], P(('gx', 'gy')), may hold values from -0.75 to 0.75
- text_gains: bfloat16 [3, 768], P(None, ('gx', 'gy')), may hold values from 0.5 to 1.5
- image_gains: bfloat16 [3, 1024], P(None, ('gx', 'gy')), may hold values from 0.5 to 1.5
- text_vectors: bfloat16 [8, 768], P(None, ('gx', 'gy')), may hold values from -3 to 3
- image_vectors: bfloat16 [8, 1024], P(None, ('gx', 'gy')), may hold values from -3 to 3
Outputs:
- text_out: bfloat16 [32, 128, 768], P(('gx', 'gy'))
- image_out: bfloat16 [32, 36, 1024], P(('gx', 'gy'))
- text_in_grad: bfloat16 [32, 128, 768], P(('gx', 'gy'))
- image_in_grad: bfloat16 [32, 36, 1024], P(('gx', 'gy'))
- co_text_proj_grad: float32 [3, 768, 1024], P(None, ('gx', 'gy'))
- co_image_proj_grad: float32 [3, 1024, 1024], P(None, ('gx', 'gy'))
- co_bias_grad: float32 [4, 1024], P(None, ('gx', 'gy'))
- co_text_out_grad: float32 [1024, 768], P(('gx', 'gy'))
- co_image_out_grad: float32 [1024, 1024], P(('gx', 'gy'))
- text_up_grad: float32 [768, 3072], P(('gx', 'gy'))
- text_up_bias_grad: float32 [3072], P(('gx', 'gy'))
- text_down_grad: float32 [3072, 768], P(('gx', 'gy'))
- image_up_grad: float32 [1024, 1024], P(('gx', 'gy'))
- image_up_bias_grad: float32 [1024], P(('gx', 'gy'))
- image_down_grad: float32 [1024, 1024], P(('gx', 'gy'))
- text_self_qkv_grad: float32 [3, 768, 768], P(None, ('gx', 'gy'))
- text_self_out_grad: float32 [768, 768], P(('gx', 'gy'))
- image_self_qkv_grad: float32 [3, 1024, 1024], P(None, ('gx', 'gy'))
- image_self_out_grad: float32 [1024, 1024], P(('gx', 'gy'))
- text_gains_grad: float32 [3, 768], P(None, ('gx', 'gy'))
- image_gains_grad: float32 [3, 1024], P(None, ('gx', 'gy'))
- text_vectors_grad: float32 [8, 768], P(None, ('gx', 'gy'))
- image_vectors_grad: float32 [8, 1024], P(None, ('gx', 'gy'))
Inputs may be any that keep to these rules, and one draw needn't show every extreme that they name: `text_lengths`: some pair has exactly 128 caption tokens and some other pair exactly 8; every other pair has 80 to 128 tokens.
All inputs are finite; a program needn't handle non-finite values. No bound on the sum of `region_mask` on one device may be relied on, other than what follows from the above.
Results may differ from a plain program's by a relative error of at most 0.025.
Values may be sent and summed in bfloat16 or wider, within the bound.
A program may use at most 256 MiB of HBM per device.

v0:
```python
import jax
import jax.numpy as jnp
from jax import lax
from jax.sharding import PartitionSpec as P

HT = 12
HV = 8
CHN = 8


EPSILON = 1e-06
MASKED = -30000.0
ROOT_HALF = 0.7071067811865476


def layer_norm(values, scale_gain, offset):
    center = values - jnp.mean(values, -1, keepdims=True)
    spread = jnp.mean(center * center, -1, keepdims=True)
    return center * lax.rsqrt(spread + EPSILON) * scale_gain + offset


def gelu_exact(values):
    return 0.5 * values * (1.0 + lax.erf(values * ROOT_HALF))


def project(inputs, weight):
    return jnp.dot(inputs, weight, preferred_element_type=jnp.float32)


def linear_back(inputs, weight, grad_low):
    weight_grad = lax.dot_general(
        inputs, grad_low, (((0,), (0,)), ((), ())), preferred_element_type=jnp.float32
    )
    input_grad = lax.dot_general(
        grad_low, weight, (((1,), (1,)), ((), ())), preferred_element_type=jnp.float32
    )
    bias_grad = jnp.sum(grad_low.astype(jnp.float32), 0)
    return (weight_grad, bias_grad, input_grad)


def split_heads(values, pair_count, head_count):
    row_count, feature_width = values.shape
    return values.reshape(
        pair_count, row_count // pair_count, head_count, feature_width // head_count
    )


def attention_scores(queries, key_rows, key_live, head_count, pair_count):
    query_heads = split_heads(queries, pair_count, head_count)
    key_heads = split_heads(key_rows, pair_count, head_count)
    score_scale = (queries.shape[1] // head_count) ** (-0.5)
    scores = (
        jnp.einsum("pqhd,pkhd->phqk", query_heads, key_heads, preferred_element_type=jnp.float32)
        * score_scale
    )
    return scores + jnp.where(key_live[:, None, None, :], 0.0, MASKED)


def attend_forward(queries, key_rows, values, key_live, head_count, pair_count):
    scores = attention_scores(queries, key_rows, key_live, head_count, pair_count)
    row_max = jnp.max(scores, -1, keepdims=True)
    log_total = row_max + jnp.log(jnp.sum(jnp.exp(scores - row_max), -1, keepdims=True))
    attention = jnp.exp(scores - log_total).astype(jnp.bfloat16)
    value_heads = split_heads(values, pair_count, head_count)
    mixture = jnp.einsum(
        "phqk,pkhd->pqhd", attention, value_heads, preferred_element_type=jnp.float32
    )
    return (mixture.reshape(queries.shape[0], values.shape[1]).astype(jnp.bfloat16), log_total)


def attend_backward(
    queries, key_rows, values, key_live, head_count, pair_count, log_total, grad_low
):
    scores = attention_scores(queries, key_rows, key_live, head_count, pair_count)
    attention = jnp.exp(scores - log_total)
    attention_low = attention.astype(jnp.bfloat16)
    query_heads = split_heads(queries, pair_count, head_count)
    key_heads = split_heads(key_rows, pair_count, head_count)
    value_heads = split_heads(values, pair_count, head_count)
    grad_heads = split_heads(grad_low, pair_count, head_count)
    value_grad = jnp.einsum(
        "phqk,pqhd->pkhd", attention_low, grad_heads, preferred_element_type=jnp.float32
    )
    attention_grad = jnp.einsum(
        "pqhd,pkhd->phqk", grad_heads, value_heads, preferred_element_type=jnp.float32
    )
    score_grad = (
        attention * (attention_grad - jnp.sum(attention * attention_grad, -1, keepdims=True))
    ).astype(jnp.bfloat16)
    score_scale = (queries.shape[1] // head_count) ** (-0.5)
    query_grad = (
        jnp.einsum("phqk,pkhd->pqhd", score_grad, key_heads, preferred_element_type=jnp.float32)
        * score_scale
    )
    key_grad = (
        jnp.einsum("phqk,pqhd->pkhd", score_grad, query_heads, preferred_element_type=jnp.float32)
        * score_scale
    )
    return (
        query_grad.reshape(queries.shape).astype(jnp.bfloat16),
        key_grad.reshape(key_rows.shape).astype(jnp.bfloat16),
        value_grad.reshape(values.shape).astype(jnp.bfloat16),
    )


def projections_back(inputs, weights, grads):
    outcomes = [linear_back(inputs, weights[position], grads[position]) for position in range(3)]
    stacked = jnp.stack([outcome[0] for outcome in outcomes])
    input_grad = outcomes[0][2] + outcomes[1][2] + outcomes[2][2]
    return (stacked, outcomes[0][1], outcomes[2][1], input_grad)


def feed_forward(normed, up_weight, up_bias, down_weight, down_bias, scale_gain, offset):
    normed_low = normed.astype(jnp.bfloat16)
    pre_act = project(normed_low, up_weight) + up_bias
    hidden, gelu_back = jax.vjp(gelu_exact, pre_act)
    hidden_low = hidden.astype(jnp.bfloat16)
    branch = project(hidden_low, down_weight) + down_bias
    second, norm_back = jax.vjp(layer_norm, normed + branch, scale_gain, offset)
    return (second, (normed_low, hidden_low, gelu_back, norm_back))


def feed_back(kept, up_weight, down_weight, grad_second):
    normed_low, hidden_low, gelu_back, norm_back = kept
    pre_grad, gain_grad, shift_grad = norm_back(grad_second)
    down_grad, down_bias_grad, hidden_grad = linear_back(
        hidden_low, down_weight, pre_grad.astype(jnp.bfloat16)
    )
    (act_grad,) = gelu_back(hidden_grad)
    up_grad, up_bias_grad, normed_grad = linear_back(
        normed_low, up_weight, act_grad.astype(jnp.bfloat16)
    )
    return (
        up_grad,
        up_bias_grad,
        down_grad,
        down_bias_grad,
        gain_grad,
        shift_grad,
        pre_grad + normed_grad,
    )


def self_block(
    second, qkv_weight, out_weight, vectors, scale_gain, key_live, head_count, pair_count
):
    second_low = second.astype(jnp.bfloat16)
    queries = (project(second_low, qkv_weight[0]) + vectors[2]).astype(jnp.bfloat16)
    key_rows = project(second_low, qkv_weight[1]).astype(jnp.bfloat16)
    values = (project(second_low, qkv_weight[2]) + vectors[3]).astype(jnp.bfloat16)
    mixture, log_total = attend_forward(queries, key_rows, values, key_live, head_count, pair_count)
    final, norm_back = jax.vjp(
        layer_norm, second + project(mixture, out_weight) + vectors[4], scale_gain, vectors[7]
    )
    return (final, (second_low, queries, key_rows, values, mixture, log_total, norm_back))


def self_back(kept, qkv_weight, out_weight, key_live, head_count, pair_count, grad_final):
    second_low, queries, key_rows, values, mixture, log_total, norm_back = kept
    pre_grad, gain_grad, shift_grad = norm_back(grad_final)
    out_grad, out_bias_grad, mixture_grad = linear_back(
        mixture, out_weight, pre_grad.astype(jnp.bfloat16)
    )
    query_grad, key_grad, value_grad = attend_backward(
        queries,
        key_rows,
        values,
        key_live,
        head_count,
        pair_count,
        log_total,
        mixture_grad.astype(jnp.bfloat16),
    )
    qkv_grad, query_bias_grad, value_bias_grad, input_grad = projections_back(
        second_low, qkv_weight, (query_grad, key_grad, value_grad)
    )
    return (
        qkv_grad,
        out_grad,
        query_bias_grad,
        value_bias_grad,
        out_bias_grad,
        gain_grad,
        shift_grad,
        pre_grad + input_grad,
    )


def per_device(
    text_in,
    image_in,
    text_lengths,
    region_mask,
    text_cot,
    image_cot,
    co_text_proj,
    co_image_proj,
    co_bias,
    co_text_out,
    co_image_out,
    text_up,
    text_up_bias,
    text_down,
    image_up,
    image_up_bias,
    image_down,
    text_self_qkv,
    text_self_out,
    image_self_qkv,
    image_self_out,
    text_gains,
    image_gains,
    text_vectors,
    image_vectors,
):
    pair_count, text_len, text_width = text_in.shape
    region_count = image_in.shape[1]
    image_width = image_in.shape[2]
    text_rows = text_in.reshape(pair_count * text_len, text_width)
    image_rows = image_in.reshape(pair_count * region_count, image_width)
    text_live = lax.broadcasted_iota(jnp.int32, (pair_count, text_len), 1) < text_lengths[:, None]
    region_live = region_mask > 0
    cross_full = (
        lax.all_gather(co_text_proj, ("gx", "gy"), axis=1, tiled=True),
        lax.all_gather(co_image_proj, ("gx", "gy"), axis=1, tiled=True),
        lax.all_gather(co_bias, ("gx", "gy"), axis=1, tiled=True),
        lax.all_gather(co_text_out, ("gx", "gy"), axis=0, tiled=True),
        lax.all_gather(co_image_out, ("gx", "gy"), axis=0, tiled=True),
        lax.all_gather(text_gains, ("gx", "gy"), axis=1, tiled=True),
        lax.all_gather(image_gains, ("gx", "gy"), axis=1, tiled=True),
        lax.all_gather(text_vectors, ("gx", "gy"), axis=1, tiled=True),
        lax.all_gather(image_vectors, ("gx", "gy"), axis=1, tiled=True),
    )
    (
        text_proj_all,
        image_proj_all,
        cross_bias_all,
        text_out_all,
        image_out_all,
        text_gain_all,
        image_gain_all,
        text_vector_all,
        image_vector_all,
    ) = cross_full
    cross_bias_float = cross_bias_all.astype(jnp.float32)
    text_gain_float = text_gain_all.astype(jnp.float32)
    image_gain_float = image_gain_all.astype(jnp.float32)
    text_vector_float = text_vector_all.astype(jnp.float32)
    image_vector_float = image_vector_all.astype(jnp.float32)
    text_query = (project(text_rows, text_proj_all[0]) + cross_bias_float[0]).astype(jnp.bfloat16)
    text_key = project(text_rows, text_proj_all[1]).astype(jnp.bfloat16)
    text_value = (project(text_rows, text_proj_all[2]) + cross_bias_float[1]).astype(jnp.bfloat16)
    image_query = (project(image_rows, image_proj_all[0]) + cross_bias_float[2]).astype(
        jnp.bfloat16
    )
    image_key = project(image_rows, image_proj_all[1]).astype(jnp.bfloat16)
    image_value = (project(image_rows, image_proj_all[2]) + cross_bias_float[3]).astype(
        jnp.bfloat16
    )
    text_mixture, text_log = attend_forward(
        text_query, image_key, image_value, region_live, CHN, pair_count
    )
    image_mixture, image_log = attend_forward(
        image_query, text_key, text_value, text_live, CHN, pair_count
    )
    text_normed, text_norm_back = jax.vjp(
        layer_norm,
        text_rows.astype(jnp.float32) + project(text_mixture, text_out_all) + text_vector_float[0],
        text_gain_float[0],
        text_vector_float[5],
    )
    image_normed, image_norm_back = jax.vjp(
        layer_norm,
        image_rows.astype(jnp.float32)
        + project(image_mixture, image_out_all)
        + image_vector_float[0],
        image_gain_float[0],
        image_vector_float[5],
    )
    feed_full = (
        lax.all_gather(text_up, ("gx", "gy"), axis=0, tiled=True),
        lax.all_gather(text_up_bias, ("gx", "gy"), axis=0, tiled=True),
        lax.all_gather(text_down, ("gx", "gy"), axis=0, tiled=True),
        lax.all_gather(image_up, ("gx", "gy"), axis=0, tiled=True),
        lax.all_gather(image_up_bias, ("gx", "gy"), axis=0, tiled=True),
        lax.all_gather(image_down, ("gx", "gy"), axis=0, tiled=True),
    )
    text_second, text_feed_kept = feed_forward(
        text_normed,
        feed_full[0],
        feed_full[1].astype(jnp.float32),
        feed_full[2],
        text_vector_float[1],
        text_gain_float[1],
        text_vector_float[6],
    )
    image_second, image_feed_kept = feed_forward(
        image_normed,
        feed_full[3],
        feed_full[4].astype(jnp.float32),
        feed_full[5],
        image_vector_float[1],
        image_gain_float[1],
        image_vector_float[6],
    )
    self_full = (
        lax.all_gather(text_self_qkv, ("gx", "gy"), axis=1, tiled=True),
        lax.all_gather(text_self_out, ("gx", "gy"), axis=0, tiled=True),
        lax.all_gather(image_self_qkv, ("gx", "gy"), axis=1, tiled=True),
        lax.all_gather(image_self_out, ("gx", "gy"), axis=0, tiled=True),
    )
    text_final, text_self_kept = self_block(
        text_second,
        self_full[0],
        self_full[1],
        text_vector_float,
        text_gain_float[2],
        text_live,
        HT,
        pair_count,
    )
    image_final, image_self_kept = self_block(
        image_second,
        self_full[2],
        self_full[3],
        image_vector_float,
        image_gain_float[2],
        region_live,
        HV,
        pair_count,
    )
    text_out = text_final.astype(jnp.bfloat16).reshape(pair_count, text_len, text_width)
    image_out = image_final.astype(jnp.bfloat16).reshape(pair_count, region_count, image_width)
    self_back_full = (
        lax.all_gather(text_self_qkv, ("gx", "gy"), axis=1, tiled=True),
        lax.all_gather(text_self_out, ("gx", "gy"), axis=0, tiled=True),
        lax.all_gather(image_self_qkv, ("gx", "gy"), axis=1, tiled=True),
        lax.all_gather(image_self_out, ("gx", "gy"), axis=0, tiled=True),
    )
    text_self_grads = self_back(
        text_self_kept,
        self_back_full[0],
        self_back_full[1],
        text_live,
        HT,
        pair_count,
        text_cot.reshape(pair_count * text_len, text_width).astype(jnp.float32),
    )
    image_self_grads = self_back(
        image_self_kept,
        self_back_full[2],
        self_back_full[3],
        region_live,
        HV,
        pair_count,
        image_cot.reshape(pair_count * region_count, image_width).astype(jnp.float32),
    )
    self_partial = (
        lax.psum_scatter(
            text_self_grads[0].astype(jnp.bfloat16), "gx", scatter_dimension=1, tiled=True
        ).astype(jnp.float32),
        lax.psum_scatter(
            text_self_grads[1].astype(jnp.bfloat16), "gx", scatter_dimension=0, tiled=True
        ).astype(jnp.float32),
        lax.psum_scatter(
            image_self_grads[0].astype(jnp.bfloat16), "gx", scatter_dimension=1, tiled=True
        ).astype(jnp.float32),
        lax.psum_scatter(
            image_self_grads[1].astype(jnp.bfloat16), "gx", scatter_dimension=0, tiled=True
        ).astype(jnp.float32),
    )
    self_sums = (
        lax.psum_scatter(
            self_partial[0].astype(jnp.bfloat16), "gy", scatter_dimension=1, tiled=True
        ).astype(jnp.float32),
        lax.psum_scatter(
            self_partial[1].astype(jnp.bfloat16), "gy", scatter_dimension=0, tiled=True
        ).astype(jnp.float32),
        lax.psum_scatter(
            self_partial[2].astype(jnp.bfloat16), "gy", scatter_dimension=1, tiled=True
        ).astype(jnp.float32),
        lax.psum_scatter(
            self_partial[3].astype(jnp.bfloat16), "gy", scatter_dimension=0, tiled=True
        ).astype(jnp.float32),
    )
    feed_back_full = (
        lax.all_gather(text_up, ("gx", "gy"), axis=0, tiled=True),
        lax.all_gather(text_down, ("gx", "gy"), axis=0, tiled=True),
        lax.all_gather(image_up, ("gx", "gy"), axis=0, tiled=True),
        lax.all_gather(image_down, ("gx", "gy"), axis=0, tiled=True),
    )
    text_feed_grads = feed_back(
        text_feed_kept, feed_back_full[0], feed_back_full[1], text_self_grads[7]
    )
    image_feed_grads = feed_back(
        image_feed_kept, feed_back_full[2], feed_back_full[3], image_self_grads[7]
    )
    feed_partial = (
        lax.psum_scatter(
            text_feed_grads[0].astype(jnp.bfloat16), "gx", scatter_dimension=0, tiled=True
        ).astype(jnp.float32),
        lax.psum_scatter(
            text_feed_grads[1].astype(jnp.bfloat16), "gx", scatter_dimension=0, tiled=True
        ).astype(jnp.float32),
        lax.psum_scatter(
            text_feed_grads[2].astype(jnp.bfloat16), "gx", scatter_dimension=0, tiled=True
        ).astype(jnp.float32),
        lax.psum_scatter(
            image_feed_grads[0].astype(jnp.bfloat16), "gx", scatter_dimension=0, tiled=True
        ).astype(jnp.float32),
        lax.psum_scatter(
            image_feed_grads[1].astype(jnp.bfloat16), "gx", scatter_dimension=0, tiled=True
        ).astype(jnp.float32),
        lax.psum_scatter(
            image_feed_grads[2].astype(jnp.bfloat16), "gx", scatter_dimension=0, tiled=True
        ).astype(jnp.float32),
    )
    feed_sums = (
        lax.psum_scatter(
            feed_partial[0].astype(jnp.bfloat16), "gy", scatter_dimension=0, tiled=True
        ).astype(jnp.float32),
        lax.psum_scatter(
            feed_partial[1].astype(jnp.bfloat16), "gy", scatter_dimension=0, tiled=True
        ).astype(jnp.float32),
        lax.psum_scatter(
            feed_partial[2].astype(jnp.bfloat16), "gy", scatter_dimension=0, tiled=True
        ).astype(jnp.float32),
        lax.psum_scatter(
            feed_partial[3].astype(jnp.bfloat16), "gy", scatter_dimension=0, tiled=True
        ).astype(jnp.float32),
        lax.psum_scatter(
            feed_partial[4].astype(jnp.bfloat16), "gy", scatter_dimension=0, tiled=True
        ).astype(jnp.float32),
        lax.psum_scatter(
            feed_partial[5].astype(jnp.bfloat16), "gy", scatter_dimension=0, tiled=True
        ).astype(jnp.float32),
    )
    cross_back_full = (
        lax.all_gather(co_text_proj, ("gx", "gy"), axis=1, tiled=True),
        lax.all_gather(co_image_proj, ("gx", "gy"), axis=1, tiled=True),
        lax.all_gather(co_text_out, ("gx", "gy"), axis=0, tiled=True),
        lax.all_gather(co_image_out, ("gx", "gy"), axis=0, tiled=True),
    )
    text_pre_grad, text_first_gain_grad, text_first_shift_grad = text_norm_back(text_feed_grads[6])
    image_pre_grad, image_first_gain_grad, image_first_shift_grad = image_norm_back(
        image_feed_grads[6]
    )
    text_out_grad, text_out_bias_grad, text_mixture_grad = linear_back(
        text_mixture, cross_back_full[2], text_pre_grad.astype(jnp.bfloat16)
    )
    image_out_grad, image_out_bias_grad, image_mixture_grad = linear_back(
        image_mixture, cross_back_full[3], image_pre_grad.astype(jnp.bfloat16)
    )
    text_query_grad, image_key_grad, image_value_grad = attend_backward(
        text_query,
        image_key,
        image_value,
        region_live,
        CHN,
        pair_count,
        text_log,
        text_mixture_grad.astype(jnp.bfloat16),
    )
    image_query_grad, text_key_grad, text_value_grad = attend_backward(
        image_query,
        text_key,
        text_value,
        text_live,
        CHN,
        pair_count,
        image_log,
        image_mixture_grad.astype(jnp.bfloat16),
    )
    text_proj_grad, text_query_bias_grad, text_value_bias_grad, text_input_grad = projections_back(
        text_rows, cross_back_full[0], (text_query_grad, text_key_grad, text_value_grad)
    )
    image_proj_grad, image_query_bias_grad, image_value_bias_grad, image_input_grad = (
        projections_back(
            image_rows, cross_back_full[1], (image_query_grad, image_key_grad, image_value_grad)
        )
    )
    cross_bias_grad = jnp.stack(
        [text_query_bias_grad, text_value_bias_grad, image_query_bias_grad, image_value_bias_grad]
    )
    text_gains_grad = jnp.stack([text_first_gain_grad, text_feed_grads[4], text_self_grads[5]])
    image_gains_grad = jnp.stack([image_first_gain_grad, image_feed_grads[4], image_self_grads[5]])
    text_vectors_grad = jnp.stack(
        [
            text_out_bias_grad,
            text_feed_grads[3],
            text_self_grads[2],
            text_self_grads[3],
            text_self_grads[4],
            text_first_shift_grad,
            text_feed_grads[5],
            text_self_grads[6],
        ]
    )
    image_vectors_grad = jnp.stack(
        [
            image_out_bias_grad,
            image_feed_grads[3],
            image_self_grads[2],
            image_self_grads[3],
            image_self_grads[4],
            image_first_shift_grad,
            image_feed_grads[5],
            image_self_grads[6],
        ]
    )
    cross_partial = (
        lax.psum_scatter(
            text_proj_grad.astype(jnp.bfloat16), "gx", scatter_dimension=1, tiled=True
        ).astype(jnp.float32),
        lax.psum_scatter(
            image_proj_grad.astype(jnp.bfloat16), "gx", scatter_dimension=1, tiled=True
        ).astype(jnp.float32),
        lax.psum_scatter(
            cross_bias_grad.astype(jnp.bfloat16), "gx", scatter_dimension=1, tiled=True
        ).astype(jnp.float32),
        lax.psum_scatter(
            text_out_grad.astype(jnp.bfloat16), "gx", scatter_dimension=0, tiled=True
        ).astype(jnp.float32),
        lax.psum_scatter(
            image_out_grad.astype(jnp.bfloat16), "gx", scatter_dimension=0, tiled=True
        ).astype(jnp.float32),
        lax.psum_scatter(
            text_gains_grad.astype(jnp.bfloat16), "gx", scatter_dimension=1, tiled=True
        ).astype(jnp.float32),
        lax.psum_scatter(
            image_gains_grad.astype(jnp.bfloat16), "gx", scatter_dimension=1, tiled=True
        ).astype(jnp.float32),
        lax.psum_scatter(
            text_vectors_grad.astype(jnp.bfloat16), "gx", scatter_dimension=1, tiled=True
        ).astype(jnp.float32),
        lax.psum_scatter(
            image_vectors_grad.astype(jnp.bfloat16), "gx", scatter_dimension=1, tiled=True
        ).astype(jnp.float32),
    )
    cross_sums = (
        lax.psum_scatter(
            cross_partial[0].astype(jnp.bfloat16), "gy", scatter_dimension=1, tiled=True
        ).astype(jnp.float32),
        lax.psum_scatter(
            cross_partial[1].astype(jnp.bfloat16), "gy", scatter_dimension=1, tiled=True
        ).astype(jnp.float32),
        lax.psum_scatter(
            cross_partial[2].astype(jnp.bfloat16), "gy", scatter_dimension=1, tiled=True
        ).astype(jnp.float32),
        lax.psum_scatter(
            cross_partial[3].astype(jnp.bfloat16), "gy", scatter_dimension=0, tiled=True
        ).astype(jnp.float32),
        lax.psum_scatter(
            cross_partial[4].astype(jnp.bfloat16), "gy", scatter_dimension=0, tiled=True
        ).astype(jnp.float32),
        lax.psum_scatter(
            cross_partial[5].astype(jnp.bfloat16), "gy", scatter_dimension=1, tiled=True
        ).astype(jnp.float32),
        lax.psum_scatter(
            cross_partial[6].astype(jnp.bfloat16), "gy", scatter_dimension=1, tiled=True
        ).astype(jnp.float32),
        lax.psum_scatter(
            cross_partial[7].astype(jnp.bfloat16), "gy", scatter_dimension=1, tiled=True
        ).astype(jnp.float32),
        lax.psum_scatter(
            cross_partial[8].astype(jnp.bfloat16), "gy", scatter_dimension=1, tiled=True
        ).astype(jnp.float32),
    )
    text_in_grad = (
        (text_pre_grad + text_input_grad)
        .astype(jnp.bfloat16)
        .reshape(pair_count, text_len, text_width)
    )
    image_in_grad = (
        (image_pre_grad + image_input_grad)
        .astype(jnp.bfloat16)
        .reshape(pair_count, region_count, image_width)
    )
    return (
        text_out,
        image_out,
        text_in_grad,
        image_in_grad,
        cross_sums[0],
        cross_sums[1],
        cross_sums[2],
        cross_sums[3],
        cross_sums[4],
        feed_sums[0],
        feed_sums[1],
        feed_sums[2],
        feed_sums[3],
        feed_sums[4],
        feed_sums[5],
        self_sums[0],
        self_sums[1],
        self_sums[2],
        self_sums[3],
        cross_sums[5],
        cross_sums[6],
        cross_sums[7],
        cross_sums[8],
    )


def solution(mesh):
    placed = (
        P(("gx", "gy"), None, None),
        P(("gx", "gy"), None, None),
        P(("gx", "gy")),
        P(("gx", "gy"), None),
        P(("gx", "gy"), None, None),
        P(("gx", "gy"), None, None),
        P(None, ("gx", "gy"), None),
        P(None, ("gx", "gy"), None),
        P(None, ("gx", "gy")),
        P(("gx", "gy"), None),
        P(("gx", "gy"), None),
        P(("gx", "gy"), None),
        P(("gx", "gy")),
        P(("gx", "gy"), None),
        P(("gx", "gy"), None),
        P(("gx", "gy")),
        P(("gx", "gy"), None),
        P(None, ("gx", "gy"), None),
        P(("gx", "gy"), None),
        P(None, ("gx", "gy"), None),
        P(("gx", "gy"), None),
        P(None, ("gx", "gy")),
        P(None, ("gx", "gy")),
        P(None, ("gx", "gy")),
        P(None, ("gx", "gy")),
    )
    return jax.shard_map(
        per_device,
        mesh=mesh,
        in_specs=placed,
        out_specs=(
            P(("gx", "gy"), None, None),
            P(("gx", "gy"), None, None),
            P(("gx", "gy"), None, None),
            P(("gx", "gy"), None, None),
            P(None, ("gx", "gy"), None),
            P(None, ("gx", "gy"), None),
            P(None, ("gx", "gy")),
            P(("gx", "gy"), None),
            P(("gx", "gy"), None),
            P(("gx", "gy"), None),
            P(("gx", "gy")),
            P(("gx", "gy"), None),
            P(("gx", "gy"), None),
            P(("gx", "gy")),
            P(("gx", "gy"), None),
            P(None, ("gx", "gy"), None),
            P(("gx", "gy"), None),
            P(None, ("gx", "gy"), None),
            P(("gx", "gy"), None),
            P(None, ("gx", "gy")),
            P(None, ("gx", "gy")),
            P(None, ("gx", "gy")),
            P(None, ("gx", "gy")),
        ),
        check_vma=False,
    )
```

profile of v0, /device:TPU:0, one launch (start us, length us, event | category | flops | bytes accessed | tf_op | source)
XLA Modules:
  0.0 2424.5 jit_solution(3418468175714607452)
XLA Ops:
  15.4 70.5 %all-gather = bf16[32,32,4]{1,2,0:T(4,128)(2,1)S(1)} all-gather(bf16[1,32,4]{1,2,0:T(4,128)(2,1)} %bitcast.719), channel_id=1, replica_groups=mesh['gx'=4,'gy'=8] {'gx','gy'}, dimensions={0}, use_global_device_ids=true | all-gather | bytes 8448 | tf_op jit(solution)/shard_map/all_gather | solution.py:226
  86.7 65.1 %all-gather.3 = bf16[32,32,8]{1,2,0:T(8,128)(2,1)S(1)} all-gather(bf16[1,32,8]{1,2,0:T(8,128)(2,1)} %bitcast.715), channel_id=1, replica_groups=mesh['gx'=4,'gy'=8] {'gx','gy'}, dimensions={0}, use_global_device_ids=true | all-gather | bytes 16896 | tf_op jit(solution)/shard_map/all_gather | solution.py:232
  151.9 65.7 %all-gather.4 = bf16[32,32,3]{1,2,0:T(4,128)(2,1)S(1)} all-gather(bf16[1,32,3]{1,2,0:T(4,128)(2,1)} %bitcast.720), channel_id=1, replica_groups=mesh['gx'=4,'gy'=8] {'gx','gy'}, dimensions={0}, use_global_device_ids=true | all-gather | bytes 6336 | tf_op jit(solution)/shard_map/all_gather | solution.py:230
  256.6 66.3 %all-gather.1 = bf16[32,24,8]{1,2,0:T(8,128)(2,1)S(1)} all-gather(bf16[1,24,8]{1,2,0:T(8,128)(2,1)S(1)} %bitcast.716), channel_id=1, replica_groups=mesh['gx'=4,'gy'=8] {'gx','gy'}, dimensions={0}, use_global_device_ids=true | all-gather | bytes 12672 | tf_op jit(solution)/shard_map/all_gather | solution.py:231
  323.3 64.6 %all-gather.2 = bf16[32,24,3]{1,2,0:T(4,128)(2,1)S(1)} all-gather(bf16[1,24,3]{1,2,0:T(4,128)(2,1)S(1)} %bitcast.721), channel_id=1, replica_groups=mesh['gx'=4,'gy'=8] {'gx','gy'}, dimensions={0}, use_global_device_ids=true | all-gather | bytes 4752 | tf_op jit(solution)/shard_map/all_gather | solution.py:229
  510.9 63.2 %all-gather.24.cloned.1.call-done = bf16[768,3072]{1,0:T(8,128)(2,1)} async-done(((bf16[24,3072]{1,0:T(8,128)(2,1)}), bf16[768,3072]{1,0:T(8,128)(2,1)}) %all-gather.24.cloned.1.call-update) | async-done | bytes 4718608 | tf_op jit(solution)/shard_map/all_gather | solution.py:281
  577.4 61.4 %all-gather.26.cloned.1.call-done = bf16[3072,768]{1,0:T(8,128)(2,1)} async-done(((bf16[96,768]{1,0:T(8,128)(2,1)}), bf16[3072,768]{1,0:T(8,128)(2,1)}) %all-gather.26.cloned.1.call-update) | async-done | bytes 4718608 | tf_op jit(solution)/shard_map/all_gather | solution.py:283
  644.2 56.0 %all-gather.28.cloned.1.call-done = bf16[3,768,768]{2,1,0:T(8,128)(2,1)} async-done(((bf16[3,24,768]{2,1,0:T(8,128)(2,1)}), bf16[3,768,768]{2,1,0:T(8,128)(2,1)}) %all-gather.28.cloned.1.call-update) | async-done | bytes 3538960 | tf_op jit(solution)/shard_map/all_gather | solution.py:307
  1203.9 50.5 %reduce-scatter.93.cloned.1.call-done = bf16[192,3072]{1,0:T(8,128)(2,1)} async-done(((bf16[768,3072]{1,0:T(8,128)(2,1)}), bf16[192,3072]{1,0:T(8,128)(2,1)}) %reduce-scatter.93.cloned.1.call-update) | async-done | bytes 1179664
  1258.7 56.0 %reduce-scatter.51.cloned.1.call-done = bf16[3,256,1024]{1,2,0:T(8,128)(2,1)} async-done(((bf16[3,1024,1024]{1,2,0:T(8,128)(2,1)}), bf16[3,256,1024]{1,2,0:T(8,128)(2,1)}) %reduce-scatter.51.cloned.1.call-update) | async-done | bytes 1572880 | tf_op jit(solution)/shard_map/reduce_scatter | solution.py:515
  1319.3 55.8 %reduce-scatter.83.cloned.1.call-done = bf16[3,256,1024]{2,1,0:T(8,128)(2,1)} async-done(((bf16[3,1024,1024]{2,1,0:T(8,128)(2,1)}), bf16[3,256,1024]{2,1,0:T(8,128)(2,1)}) %reduce-scatter.83.cloned.1.call-update) | async-done | bytes 1572880 | tf_op jit(solution)/shard_map/reduce_scatter | solution.py:365
  1401.1 62.7 %reduce-scatter.105.cloned.1.call-done = bf16[32,3]{1,0:T(8,128)(2,1)} async-done(((bf16[256,3]{1,0:T(8,128)(2,1)}), bf16[32,3]{1,0:T(8,128)(2,1)}) %reduce-scatter.105.cloned.1.call-update) | async-done | bytes 208
  1465.2 63.4 %reduce-scatter.97.cloned.1.call-done = bf16[32,4]{1,0:T(8,128)(2,1)} async-done(((bf16[256,4]{1,0:T(8,128)(2,1)}), bf16[32,4]{1,0:T(8,128)(2,1)}) %reduce-scatter.97.cloned.1.call-update) | async-done | bytes 272
  1618.3 60.4 %reduce-scatter.81.cloned.1.call-done = bf16[24,768]{1,0:T(8,128)(2,1)} async-done(((bf16[192,768]{1,0:T(8,128)(2,1)}), bf16[24,768]{1,0:T(8,128)(2,1)}) %reduce-scatter.81.cloned.1.call-update) | async-done | bytes 36880 | tf_op jit(solution)/shard_map/reduce_scatter | solution.py:376
  1680.1 63.1 %reduce-scatter.55.cloned.1.call-done = bf16[32,768]{1,0:T(8,128)(2,1)} async-done(((bf16[256,768]{1,0:T(8,128)(2,1)}), bf16[32,768]{1,0:T(8,128)(2,1)}) %reduce-scatter.55.cloned.1.call-update) | async-done | bytes 49168 | tf_op jit(solution)/shard_map/reduce_scatter | solution.py:550
  1744.6 63.6 %reduce-scatter.71.cloned.1.call-done = bf16[32,1024]{1,0:T(8,128)(2,1)} async-done(((bf16[256,1024]{1,0:T(8,128)(2,1)}), bf16[32,1024]{1,0:T(8,128)(2,1)}) %reduce-scatter.71.cloned.1.call-update) | async-done | bytes 65552 | tf_op jit(solution)/shard_map/reduce_scatter | solution.py:428
  1809.7 63.4 %reduce-scatter.75.cloned.1.call-done = bf16[32,1024]{1,0:T(8,128)(2,1)} async-done(((bf16[256,1024]{1,0:T(8,128)(2,1)}), bf16[32,1024]{1,0:T(8,128)(2,1)}) %reduce-scatter.75.cloned.1.call-update) | async-done | bytes 65552 | tf_op jit(solution)/shard_map/reduce_scatter | solution.py:434
  1874.6 63.4 %reduce-scatter.89.cloned.1.call-done = bf16[32,1024]{1,0:T(8,128)(2,1)} async-done(((bf16[256,1024]{1,0:T(8,128)(2,1)}), bf16[32,1024]{1,0:T(8,128)(2,1)}) %reduce-scatter.89.cloned.1.call-update) | async-done | bytes 65552 | tf_op jit(solution)/shard_map/reduce_scatter | solution.py:382
  1939.6 63.5 %reduce-scatter.59.cloned.1.call-done = bf16[32,1024]{1,0:T(8,128)(2,1)} async-done(((bf16[256,1024]{1,0:T(8,128)(2,1)}), bf16[32,1024]{1,0:T(8,128)(2,1)}) %reduce-scatter.59.cloned.1.call-update) | async-done | bytes 65552 | tf_op jit(solution)/shard_map/reduce_scatter | solution.py:553
  2004.6 63.0 %reduce-scatter.99.cloned.1.call-done = bf16[24,2304]{1,0:T(8,128)(2,1)} async-done(((bf16[192,2304]{1,0:T(8,128)(2,1)}), bf16[24,2304]{1,0:T(8,128)(2,1)}) %reduce-scatter.99.cloned.1.call-update) | async-done | bytes 110608
  2069.2 65.3 %reduce-scatter.63.cloned.1.call-done = bf16[24,3072]{1,0:T(8,128)(2,1)} async-done(((bf16[192,3072]{1,0:T(8,128)(2,1)}), bf16[24,3072]{1,0:T(8,128)(2,1)}) %reduce-scatter.63.cloned.1.call-update) | async-done | bytes 147472 | tf_op jit(solution)/shard_map/reduce_scatter | solution.py:419
  2136.1 65.6 %reduce-scatter.67.cloned.1.call-done = bf16[96,768]{1,0:T(8,128)(2,1)} async-done(((bf16[768,768]{1,0:T(8,128)(2,1)}), bf16[96,768]{1,0:T(8,128)(2,1)}) %reduce-scatter.67.cloned.1.call-update) | async-done | bytes 147472 | tf_op jit(solution)/shard_map/reduce_scatter | solution.py:425
  2203.4 144.1 %all-reduce.16.cloned.1.call-done = (bf16[3,192,1024]{2,0,1:T(4,128)(2,1)}, bf16[3,256,1024]{2,0,1:T(4,128)(2,1)}) async-done(((bf16[3,192,1024]{2,0,1:T(4,128)(2,1)}, bf16[3,256,1024]{2,0,1:T(4,128)(2,1)}), (bf16[3,192,1024]{2,0,1:T(4,128)(2,1)}, bf16[3,256,1024]{2,0,1:T(4,128)(2,1)})) %all-reduce.16.cloned.1.call-update) | async-done | bytes 2752528
  2351.3 64.5 %reduce-scatter.85.cloned.1.call-done = bf16[3,32,1024]{2,1,0:T(8,128)(2,1)} async-done(((bf16[3,256,1024]{2,1,0:T(8,128)(2,1)}), bf16[3,32,1024]{2,1,0:T(8,128)(2,1)}) %reduce-scatter.85.cloned.1.call-update) | async-done | bytes 196624 | tf_op jit(solution)/shard_map/reduce_scatter | solution.py:379
  (747 shorter events, 821.5 us)
Async XLA Ops:
  12.0 496.8 %all-gather.22.cloned.1.call-start = ((), (), s32[]{:S(2)}) async-start(), calls=%async_computation.32 | async-start | bytes 1622016 | tf_op jit(solution)/shard_map/all_gather | solution.py:227
  12.7 561.4 %all-gather.24.cloned.1.call-start = ((), (), s32[]{:S(2)}) async-start(), calls=%async_computation.33 | async-start | bytes 4866048 | tf_op jit(solution)/shard_map/all_gather | solution.py:281
  13.5 625.3 %all-gather.26.cloned.1.call-start = ((), (), s32[]{:S(2)}) async-start(), calls=%async_computation.34 | async-start | bytes 4866048 | tf_op jit(solution)/shard_map/all_gather | solution.py:283
  14.0 686.1 %all-gather.28.cloned.1.call-start = ((), (), s32[]{:S(2)}) async-start(), calls=%async_computation.35 | async-start | bytes 3649536 | tf_op jit(solution)/shard_map/all_gather | solution.py:307
  14.8 741.1 %all-gather.30.cloned.1.call-start = ((), (), s32[]{:S(2)}) async-start(), calls=%async_computation.36 | async-start | bytes 1216512 | tf_op jit(solution)/shard_map/all_gather | solution.py:308
  15.4 860.8 %reduce-scatter.103.cloned.1.call-start = ((), (), s32[]{:S(2)}) async-start(), calls=%async_computation.68 | async-start | bytes 327680
  861.3 453.5 %reduce-scatter.51.cloned.1.call-start = ((), (), s32[]{:S(2)}) async-start(), calls=%async_computation.42 | async-start | bytes 7864320 | tf_op jit(solution)/shard_map/reduce_scatter | solution.py:515
  868.1 507.0 %reduce-scatter.83.cloned.1.call-start = ((), (), s32[]{:S(2)}) async-start(), calls=%async_computation.58 | async-start | bytes 7864320 | tf_op jit(solution)/shard_map/reduce_scatter | solution.py:365
  874.6 525.6 %reduce-scatter.101.cloned.1.call-start = ((), (), s32[]{:S(2)}) async-start(), calls=%async_computation.67 | async-start | bytes 245760
  876.1 587.7 %reduce-scatter.105.cloned.1.call-start = ((), (), s32[]{:S(2)}) async-start(), calls=%async_computation.69 | async-start | bytes 73728
  876.8 651.7 %reduce-scatter.97.cloned.1.call-start = ((), (), s32[]{:S(2)}) async-start(), calls=%async_computation.65 | async-start | bytes 73728
  877.4 673.0 %reduce-scatter.107.cloned.1.call-start = ((), (), s32[]{:S(2)}) async-start(), calls=%async_computation.70 | async-start | bytes 245760
  878.7 738.2 %reduce-scatter.109.cloned.1.call-start = ((), (), s32[]{:S(2)}) async-start(), calls=%async_computation.71 | async-start | bytes 73728
  880.2 798.4 %reduce-scatter.81.cloned.1.call-start = ((), (), s32[]{:S(2)}) async-start(), calls=%async_computation.57 | async-start | bytes 331776 | tf_op jit(solution)/shard_map/reduce_scatter | solution.py:376
  895.1 848.1 %reduce-scatter.55.cloned.1.call-start = ((), (), s32[]{:S(2)}) async-start(), calls=%async_computation.44 | async-start | bytes 442368 | tf_op jit(solution)/shard_map/reduce_scatter | solution.py:550
  925.5 882.7 %reduce-scatter.71.cloned.1.call-start = ((), (), s32[]{:S(2)}) async-start(), calls=%async_computation.52 | async-start | bytes 589824 | tf_op jit(solution)/shard_map/reduce_scatter | solution.py:428
  959.1 914.0 %reduce-scatter.75.cloned.1.call-start = ((), (), s32[]{:S(2)}) async-start(), calls=%async_computation.54 | async-start | bytes 589824 | tf_op jit(solution)/shard_map/reduce_scatter | solution.py:434
  992.8 945.2 %reduce-scatter.89.cloned.1.call-start = ((), (), s32[]{:S(2)}) async-start(), calls=%async_computation.61 | async-start | bytes 589824 | tf_op jit(solution)/shard_map/reduce_scatter | solution.py:382
  1026.4 976.7 %reduce-scatter.59.cloned.1.call-start = ((), (), s32[]{:S(2)}) async-start(), calls=%async_computation.46 | async-start | bytes 589824 | tf_op jit(solution)/shard_map/reduce_scatter | solution.py:553
  1060.1 1007.5 %reduce-scatter.99.cloned.1.call-start = ((), (), s32[]{:S(2)}) async-start(), calls=%async_computation.66 | async-start | bytes 995328
  1105.9 1028.6 %reduce-scatter.63.cloned.1.call-start = ((), (), s32[]{:S(2)}) async-start(), calls=%async_computation.48 | async-start | bytes 1327104 | tf_op jit(solution)/shard_map/reduce_scatter | solution.py:419
  1153.5 1048.3 %reduce-scatter.67.cloned.1.call-start = ((), (), s32[]{:S(2)}) async-start(), calls=%async_computation.50 | async-start | bytes 1327104 | tf_op jit(solution)/shard_map/reduce_scatter | solution.py:425
  1203.9 1143.6 %all-reduce.16.cloned.1.call-start = ((), (), s32[]{:S(2)}) async-start(), calls=%async_computation.72 | async-start | bytes 7340032
  1319.2 1096.6 %reduce-scatter.85.cloned.1.call-start = ((), (), s32[]{:S(2)}) async-start(), calls=%async_computation.59 | async-start | bytes 1769472 | tf_op jit(solution)/shard_map/reduce_scatter | solution.py:379
  (192 other events, 11996.1 us)
Sparse Core Ops, SparseCore 0:
  10.9 66.4 all-gather.19
  80.4 67.7 all-gather.17
  209.0 55.7 all-gather.33
  267.6 55.1 all-gather.35
  325.7 68.1 all-gather.37
  511.7 62.4 all-gather.23
  576.9 61.8 all-gather.25
  641.7 58.4 all-gather.27
  1256.8 57.8 reduce-scatter.50
  1317.1 57.9 reduce-scatter.82
  1401.3 62.4 reduce-scatter.104
  1467.1 61.4 reduce-scatter.96
  1554.4 62.4 reduce-scatter.108
  1620.1 58.5 reduce-scatter.80
  1681.9 61.2 reduce-scatter.54
  1746.5 61.6 reduce-scatter.70
  1811.4 61.6 reduce-scatter.74
  1876.3 61.6 reduce-scatter.88
  1941.4 61.6 reduce-scatter.58
  2006.4 61.1 reduce-scatter.98
  2071.0 63.4 reduce-scatter.62
  2137.9 63.8 reduce-scatter.66
  2205.5 141.9 all-reduce.15
  2350.7 64.9 reduce-scatter.84
  (19 shorter events, 675.0 us)
where the time goes:
time: 2430 us; the launch traced here: 2420 us
  waiting for transfers between devices  1760 us (72%)
  blocking collectives  398 us (16%)
  matrix products  132 us (5%)
  local copies, waits for them, and re-layouts  65.7 us (3%)
  other arithmetic  42.5 us (2%)
    unnamed x53, waiting for transfers between devices  454 us
    all_gather x1, blocking collectives, per_device(): lax.all_gather(co_bias, ('gx', 'gy'), axis=1, tiled=True)  70.5 us
    all_gather x1, blocking collectives, per_device(): lax.all_gather(text_vectors, ('gx', 'gy'), axis=1, tiled=True)  66.3 us
    all_gather x1, blocking collectives, per_device(): lax.all_gather(image_gains, ('gx', 'gy'), axis=1, tiled=True)  65.7 us
    reduce_scatter x1, waiting for transfers between devices, per_device(): lax.psum_scatter(feed_partial[2].astype(jnp.bfloat16), 'gy', scatter_dime...  65.6 us
    unnamed x3, blocking collectives  65.4 us
    reduce_scatter x1, waiting for transfers between devices, per_device(): lax.psum_scatter(feed_partial[0].astype(jnp.bfloat16), 'gy', scatter_dime...  65.3 us
    all_gather x1, blocking collectives, per_device(): lax.all_gather(image_vectors, ('gx', 'gy'), axis=1, tiled=True)  65.1 us
  transfers between devices with their start and end apart: 43, of which 33 were waited for; matrix products, arithmetic and copies ran while one was open for 8% of the time, Pallas kernels for 0%

commit v1 on v0

--- a/solution.py
+++ b/solution.py
@@ -1,7 +1,159 @@
+import functools
+
 import jax
 import jax.numpy as jnp
 from jax import lax
+from jax.experimental import pallas as pl
+from jax.experimental.pallas import tpu as pltpu
 from jax.sharding import PartitionSpec as P
+
+MESH = pl.DeviceIdType.MESH
+ORDERS = ((2, 0, 1), (2, 1, 0))
+
+def place_of(sizes):
+    X, Y, Z = sizes
+    gx, gy = lax.axis_index("gx"), lax.axis_index("gy")
+    return (gx // 2, gy % Y, gy // Y), gx % 2
+
+def device_of(sizes, place, core):
+    return (place[0] * 2 + core, place[2] * sizes[1] + place[1])
+
+def shifted(sizes, place, dim, step):
+    return tuple(lax.rem(p + step, sizes[dim]) if i == dim else p for i, p in enumerate(place))
+
+def greet(sizes, place, core):
+    barrier = pltpu.get_barrier_semaphore()
+    count = 1
+    pl.semaphore_signal(barrier, inc=1, device_id=device_of(sizes, place, 1 - core), device_id_type=MESH)
+    for dim in range(3):
+        for step in range(1, sizes[dim]):
+            pl.semaphore_signal(barrier, inc=1, device_id=device_of(sizes, shifted(sizes, place, dim, step), core), device_id_type=MESH)
+            count += 1
+    pl.semaphore_wait(barrier, count)
+
+def slot_base(sizes):
+    return {0: 0, 1: sizes[0] - 1, 2: sizes[0] + sizes[1] - 2}
+
+def gather_kernel(sizes, pieces, ahead, *refs):
+    n_in = max(p[0] for p in pieces) + 1
+    n = len(pieces)
+    ins, outs = refs[:n_in], refs[n_in:n_in + n]
+    send, recv, own = refs[n_in + n:]
+    place, core = place_of(sizes)
+    x, y, z = place
+    base = slot_base(sizes)
+    last = sum(sizes) - 3
+    greet(sizes, place, core)
+    def src_of(m):
+        number, index, _ = pieces[m]
+        return ins[number] if index is None else ins[number].at[index]
+    keep = []
+    for m in range(n):
+        copy = pltpu.make_async_copy(src_of(m), outs[m].at[x, core, z, y], own.at[m])
+        copy.start()
+        keep.append(copy)
+    def view(m, where, opened):
+        px, py, pz = (slice(None) if d in opened else where[d] for d in range(3))
+        return outs[m].at[px, core, pz, py]
+    started = []
+    arrive = {}
+    def start(m, phase):
+        order = ORDERS[pieces[m][2]]
+        waits = []
+        if phase == 3:
+            part = outs[m].at[:, core]
+            copy = pltpu.make_async_remote_copy(part, part, send.at[m, last], recv.at[m, last],
+                device_id=device_of(sizes, place, 1 - core), device_id_type=MESH)
+            copy.start()
+            started.append(copy)
+            waits.append(pltpu.make_async_remote_copy(outs[m].at[:, 1 - core], outs[m].at[:, 1 - core], send.at[m, last], recv.at[m, last],
+                device_id=device_of(sizes, place, 1 - core), device_id_type=MESH))
+        else:
+            dim = order[phase]
+            opened = order[:phase]
+            part = view(m, place, opened)
+            source = src_of(m) if phase == 0 else part
+            for step in range(1, sizes[dim]):
+                slot = base[dim] + step - 1
+                peer = shifted(sizes, place, dim, step)
+                back = shifted(sizes, place, dim, sizes[dim] - step)
+                copy = pltpu.make_async_remote_copy(source, part, send.at[m, slot], recv.at[m, slot],
+                    device_id=device_of(sizes, peer, core), device_id_type=MESH)
+                copy.start()
+                started.append(copy)
+                came = view(m, back, opened)
+                waits.append(pltpu.make_async_remote_copy(came, came, send.at[m, slot], recv.at[m, slot],
+                    device_id=device_of(sizes, peer, core), device_id_type=MESH))
+        arrive[m, phase] = waits
+    def settle(m, phase):
+        for w in arrive[m, phase]:
+            w.wait_recv()
+    for s in range(n + 3 + ahead):
+        if s < n:
+            start(s, 0)
+        for phase in (1, 2, 3):
+            m = s - ahead - phase + 1
+            if 0 <= m < n:
+                settle(m, phase - 1)
+                if phase == 1:
+                    keep[m].wait()
+                start(m, phase)
+    for m in range(n):
+        settle(m, 3)
+    for c in started:
+        c.wait_send()
+
+def gather(sizes, inputs, pieces, ahead=3, collective_id=0):
+    X, Y, Z = sizes
+    outs = []
+    for number, index, _ in pieces:
+        a = inputs[number]
+        outs.append(jax.ShapeDtypeStruct((X, 2, Z, Y) + a.shape[(0 if index is None else 1):], a.dtype))
+    n = len(pieces)
+    slots = sum(sizes) - 2
+    return pl.pallas_call(
+        functools.partial(gather_kernel, sizes, pieces, ahead),
+        out_shape=outs,
+        in_specs=[pl.BlockSpec(memory_space=pl.ANY)] * len(inputs),
+        out_specs=[pl.BlockSpec(memory_space=pl.ANY)] * n,
+        scratch_shapes=[pltpu.SemaphoreType.DMA((n, slots)), pltpu.SemaphoreType.DMA((n, slots)), pltpu.SemaphoreType.DMA((n,))],
+        compiler_params=pltpu.CompilerParams(collective_id=collective_id, has_side_effects=True),
+    )(*inputs)
+
+def mesh_sizes(mesh):
+    ys = len({d.coords[1] for d in mesh.devices.flat})
+    return (mesh.shape["gx"] // 2, ys, mesh.shape["gy"] // ys)
+
+
+def pack_small(small):
+    flat = jnp.concatenate([a.reshape(-1) for a in small])
+    return jnp.pad(flat, (0, 1024 - flat.shape[0])).reshape(8, 128)
+
+
+def unpack_small(full, small):
+    count = full.shape[0] // 8
+    rows = full.reshape(count, 1024)
+    outs, at = [], 0
+    for a in small:
+        part = rows[:, at:at + a.size]
+        at += a.size
+        if a.ndim == 1:
+            outs.append(part.reshape(-1))
+        else:
+            part = part.reshape(count, *a.shape).transpose(1, 0, 2)
+            outs.append(part.reshape(a.shape[0], -1))
+    return outs
+
+
+def gather_all(sizes, packed, big):
+    inputs = (packed, *big)
+    pieces = [(0, None, 0)]
+    for number, a in enumerate(big):
+        for index in range(3) if a.ndim == 3 else (None,):
+            pieces.append((number + 1, index, len(pieces) % 2))
+    outs = gather(sizes, inputs, pieces)
+    return [o.reshape(-1, o.shape[-1]) for o in outs]
+
 
 HT = 12
 HV = 8
@@ -187,6 +339,7 @@
 
 
 def per_device(
+    sizes,
     text_in,
     image_in,
     text_lengths,
@@ -220,28 +373,20 @@
     image_rows = image_in.reshape(pair_count * region_count, image_width)
     text_live = lax.broadcasted_iota(jnp.int32, (pair_count, text_len), 1) < text_lengths[:, None]
     region_live = region_mask > 0
-    cross_full = (
-        lax.all_gather(co_text_proj, ("gx", "gy"), axis=1, tiled=True),
-        lax.all_gather(co_image_proj, ("gx", "gy"), axis=1, tiled=True),
-        lax.all_gather(co_bias, ("gx", "gy"), axis=1, tiled=True),
-        lax.all_gather(co_text_out, ("gx", "gy"), axis=0, tiled=True),
-        lax.all_gather(co_image_out, ("gx", "gy"), axis=0, tiled=True),
-        lax.all_gather(text_gains, ("gx", "gy"), axis=1, tiled=True),
-        lax.all_gather(image_gains, ("gx", "gy"), axis=1, tiled=True),
-        lax.all_gather(text_vectors, ("gx", "gy"), axis=1, tiled=True),
-        lax.all_gather(image_vectors, ("gx", "gy"), axis=1, tiled=True),
-    )
+    small = (co_bias, text_gains, image_gains, text_vectors, image_vectors, text_up_bias, image_up_bias)
+    big = (
+        co_text_proj, co_image_proj, co_text_out, co_image_out, text_up, text_down, image_up, image_down,
+        text_self_qkv, text_self_out, image_self_qkv, image_self_out,
+    )
+    full = gather_all(sizes, pack_small(small), big)
     (
-        text_proj_all,
-        image_proj_all,
-        cross_bias_all,
-        text_out_all,
-        image_out_all,
-        text_gain_all,
-        image_gain_all,
-        text_vector_all,
-        image_vector_all,
-    ) = cross_full
+        cross_bias_all, text_gain_all, image_gain_all, text_vector_all, image_vector_all,
+        text_up_bias_all, image_up_bias_all,
+    ) = unpack_small(full[0], small)
+    text_proj_all, image_proj_all = full[1:4], full[4:7]
+    text_out_all, image_out_all = full[7], full[8]
+    feed_full = (full[9], text_up_bias_all, full[10], full[11], image_up_bias_all, full[12])
+    self_full = (full[13:16], full[16], full[17:20], full[20])
     cross_bias_float = cross_bias_all.astype(jnp.float32)
     text_gain_float = text_gain_all.astype(jnp.float32)
     image_gain_float = image_gain_all.astype(jnp.float32)
@@ -277,14 +422,6 @@
         image_gain_float[0],
         image_vector_float[5],
     )
-    feed_full = (
-        lax.all_gather(text_up, ("gx", "gy"), axis=0, tiled=True),
-        lax.all_gather(text_up_bias, ("gx", "gy"), axis=0, tiled=True),
-        lax.all_gather(text_down, ("gx", "gy"), axis=0, tiled=True),
-        lax.all_gather(image_up, ("gx", "gy"), axis=0, tiled=True),
-        lax.all_gather(image_up_bias, ("gx", "gy"), axis=0, tiled=True),
-        lax.all_gather(image_down, ("gx", "gy"), axis=0, tiled=True),
-    )
     text_second, text_feed_kept = feed_forward(
         text_normed,
         feed_full[0],
@@ -302,12 +439,6 @@
         image_vector_float[1],
         image_gain_float[1],
         image_vector_float[6],
-    )
-    self_full = (
-        lax.all_gather(text_self_qkv, ("gx", "gy"), axis=1, tiled=True),
-        lax.all_gather(text_self_out, ("gx", "gy"), axis=0, tiled=True),
-        lax.all_gather(image_self_qkv, ("gx", "gy"), axis=1, tiled=True),
-        lax.all_gather(image_self_out, ("gx", "gy"), axis=0, tiled=True),
     )
     text_final, text_self_kept = self_block(
         text_second,
@@ -331,16 +462,10 @@
     )
     text_out = text_final.astype(jnp.bfloat16).reshape(pair_count, text_len, text_width)
     image_out = image_final.astype(jnp.bfloat16).reshape(pair_count, region_count, image_width)
-    self_back_full = (
-        lax.all_gather(text_self_qkv, ("gx", "gy"), axis=1, tiled=True),
-        lax.all_gather(text_self_out, ("gx", "gy"), axis=0, tiled=True),
-        lax.all_gather(image_self_qkv, ("gx", "gy"), axis=1, tiled=True),
-        lax.all_gather(image_self_out, ("gx", "gy"), axis=0, tiled=True),
-    )
     text_self_grads = self_back(
         text_self_kept,
-        self_back_full[0],
-        self_back_full[1],
+        self_full[0],
+        self_full[1],
         text_live,
         HT,
         pair_count,
@@ -348,8 +473,8 @@
     )
     image_self_grads = self_back(
         image_self_kept,
-        self_back_full[2],
-        self_back_full[3],
+        self_full[2],
+        self_full[3],
         region_live,
         HV,
         pair_count,
@@ -383,17 +508,11 @@
             self_partial[3].astype(jnp.bfloat16), "gy", scatter_dimension=0, tiled=True
         ).astype(jnp.float32),
     )
-    feed_back_full = (
-        lax.all_gather(text_up, ("gx", "gy"), axis=0, tiled=True),
-        lax.all_gather(text_down, ("gx", "gy"), axis=0, tiled=True),
-        lax.all_gather(image_up, ("gx", "gy"), axis=0, tiled=True),
-        lax.all_gather(image_down, ("gx", "gy"), axis=0, tiled=True),
-    )
     text_feed_grads = feed_back(
-        text_feed_kept, feed_back_full[0], feed_back_full[1], text_self_grads[7]
+        text_feed_kept, feed_full[0], feed_full[2], text_self_grads[7]
     )
     image_feed_grads = feed_back(
-        image_feed_kept, feed_back_full[2], feed_back_full[3], image_self_grads[7]
+        image_feed_kept, feed_full[3], feed_full[5], image_self_grads[7]
     )
     feed_partial = (
         lax.psum_scatter(
@@ -434,22 +553,16 @@
         lax.psum_scatter(
             feed_partial[5].astype(jnp.bfloat16), "gy", scatter_dimension=0, tiled=True
         ).astype(jnp.float32),
-    )
-    cross_back_full = (
-        lax.all_gather(co_text_proj, ("gx", "gy"), axis=1, tiled=True),
-        lax.all_gather(co_image_proj, ("gx", "gy"), axis=1, tiled=True),
-        lax.all_gather(co_text_out, ("gx", "gy"), axis=0, tiled=True),
-        lax.all_gather(co_image_out, ("gx", "gy"), axis=0, tiled=True),
     )
     text_pre_grad, text_first_gain_grad, text_first_shift_grad = text_norm_back(text_feed_grads[6])
     image_pre_grad, image_first_gain_grad, image_first_shift_grad = image_norm_back(
         image_feed_grads[6]
     )
     text_out_grad, text_out_bias_grad, text_mixture_grad = linear_back(
-        text_mixture, cross_back_full[2], text_pre_grad.astype(jnp.bfloat16)
+        text_mixture, text_out_all, text_pre_grad.astype(jnp.bfloat16)
     )
     image_out_grad, image_out_bias_grad, image_mixture_grad = linear_back(
-        image_mixture, cross_back_full[3], image_pre_grad.astype(jnp.bfloat16)
+        image_mixture, image_out_all, image_pre_grad.astype(jnp.bfloat16)
     )
     text_query_grad, image_key_grad, image_value_grad = attend_backward(
         text_query,
@@ -472,11 +585,11 @@
         image_mixture_grad.astype(jnp.bfloat16),
     )
     text_proj_grad, text_query_bias_grad, text_value_bias_grad, text_input_grad = projections_back(
-        text_rows, cross_back_full[0], (text_query_grad, text_key_grad, text_value_grad)
+        text_rows, text_proj_all, (text_query_grad, text_key_grad, text_value_grad)
     )
     image_proj_grad, image_query_bias_grad, image_value_bias_grad, image_input_grad = (
         projections_back(
-            image_rows, cross_back_full[1], (image_query_grad, image_key_grad, image_value_grad)
+            image_rows, image_proj_all, (image_query_grad, image_key_grad, image_value_grad)
         )
     )
     cross_bias_grad = jnp.stack(
@@ -632,7 +745,7 @@
         P(None, ("gx", "gy")),
     )
     return jax.shard_map(
-        per_device,
+        functools.partial(per_device, mesh_sizes(mesh)),
         mesh=mesh,
         in_specs=placed,
         out_specs=(

time: 2430 us -> 1940 us (0.80)
  blocking collectives: 398 us -> 27.8 us
  waiting for transfers between devices: 1760 us -> 1440 us
  Pallas kernels: 0 us -> 194 us
  matrix products: 132 us -> 105 us
    all_gather x5 -> x0, blocking collectives: 332 us -> none  [the longest x1 70.5 us: per_device(): lax.all_gather(co_bias, ('gx', 'gy'), axis=1, tiled=True)]
    all_gather x12 -> x0, waiting for transfers between devices: 303 us -> none  [the longest x1 63.2 us: per_device(): lax.all_gather(text_up, ('gx', 'gy'), axis=0, tiled=True)]
    pallas_call x0 -> x1, Pallas kernels: none -> 194 us  [gather(): pl.pallas_call(functools.partial(gather_kernel, sizes, pieces, ahead), ou...]
    unnamed x3 -> x2, blocking collectives: 65.4 us -> 27.8 us
    unnamed x398 -> x416, local copies, waits for them, and re-layouts: 49.4 us -> 53.1 us
    unnamed x53 -> x41, waiting for transfers between devices: 454 us -> 453 us
  transfers between devices with their start and end apart: 43 -> 31, of which waited for: 33 -> 28; matrix products, arithmetic and copies ran while one was open for 8% -> 9% of each run, Pallas kernels for 0% -> 0%
where the time goes in v1:
time: 1940 us; the launch traced here: 1930 us
  waiting for transfers between devices  1440 us (74%)
  Pallas kernels  194 us (10%)
  matrix products  105 us (5%)
  local copies, waits for them, and re-layouts  87.1 us (4%)
  other arithmetic  50.1 us (3%)
  blocking collectives  27.8 us (1%)
  between operations  21.9 us (1%)
    unnamed x41, waiting for transfers between devices  453 us
    pallas_call x1, Pallas kernels, gather(): pl.pallas_call(functools.partial(gather_kernel, sizes, pieces, ahead), ou...  194 us
    reduce_scatter x1, waiting for transfers between devices, per_device(): lax.psum_scatter(feed_partial[2].astype(jnp.bfloat16), 'gy', scatter_dime...  65.5 us
    reduce_scatter x1, waiting for transfers between devices, per_device(): lax.psum_scatter(feed_partial[0].astype(jnp.bfloat16), 'gy', scatter_dime...  65.4 us
    reduce_scatter x1, waiting for transfers between devices, per_device(): lax.psum_scatter(self_partial[2].astype(jnp.bfloat16), 'gy', scatter_dime...  64.6 us
    reduce_scatter x1, waiting for transfers between devices, per_device(): lax.psum_scatter(feed_partial[3].astype(jnp.bfloat16), 'gy', scatter_dime...  63.6 us
    reduce_scatter x1, waiting for transfers between devices, per_device(): lax.psum_scatter(self_partial[3].astype(jnp.bfloat16), 'gy', scatter_dime...  63.5 us
    reduce_scatter x1, waiting for transfers between devices, per_device(): lax.psum_scatter(cross_partial[4].astype(jnp.bfloat16), 'gy', scatter_dim...  63.4 us
  transfers between devices with their start and end apart: 31, of which 28 were waited for; matrix products, arithmetic and copies ran while one was open for 9% of the time, Pallas kernels for 0%

profile of v1, /device:TPU:0, one launch (start us, length us, event | category | flops | bytes accessed | tf_op | source)
XLA Modules:
  0.0 1932.9 jit_solution(9583293598121457181)
XLA Ops:
  13.1 194.3 %shard_map.416 = (bf16[2,2,4,2,8,128]{5,4,3,2,1,0:T(8,128)(2,1)}, bf16[2,2,4,2,24,1024]{5,4,3,2,1,0:T(8,128)(2,1)}, bf16[2,2,4,2,24,1024]{5,4,3,2,1,0:T(8,128)(2...) custom-call(bf16[8,128]{1,0:T(8,128)(2,1)} %pad_bitcast_fusion.refs_, ...), custom_call_target="tpu_custom_call" | custom-call | tf_op jit(solution)/shard_map/pallas_call | solution.py:114
  468.0 33.7 %reduce-scatter.73.cloned.1.call-done = bf16[256,1024]{1,0:T(8,128)(2,1)} async-done(((bf16[1024,1024]{1,0:T(8,128)(2,1)}), bf16[256,1024]{1,0:T(8,128)(2,1)}) %reduce-scatter.73.cloned.1.call-update) | async-done | bytes 524304 | tf_op jit(solution)/shard_map/reduce_scatter | solution.py:533
  501.7 33.6 %reduce-scatter.87.cloned.1.call-done = bf16[256,1024]{1,0:T(8,128)(2,1)} async-done(((bf16[1024,1024]{1,0:T(8,128)(2,1)}), bf16[256,1024]{1,0:T(8,128)(2,1)}) %reduce-scatter.87.cloned.1.call-update) | async-done | bytes 524304 | tf_op jit(solution)/shard_map/reduce_scatter | solution.py:493
  535.4 33.7 %reduce-scatter.57.cloned.1.call-done = bf16[256,1024]{1,0:T(8,128)(2,1)} async-done(((bf16[1024,1024]{1,0:T(8,128)(2,1)}), bf16[256,1024]{1,0:T(8,128)(2,1)}) %reduce-scatter.57.cloned.1.call-update) | async-done | bytes 524304 | tf_op jit(solution)/shard_map/reduce_scatter | solution.py:637
  569.2 42.6 %reduce-scatter.77.cloned.1.call-done = bf16[3,192,768]{2,1,0:T(8,128)(2,1)} async-done(((bf16[3,768,768]{2,1,0:T(8,128)(2,1)}), bf16[3,192,768]{2,1,0:T(8,128)(2,1)}) %reduce-scatter.77.cloned.1.call-update) | async-done | bytes 884752 | tf_op jit(solution)/shard_map/reduce_scatter | solution.py:484
  614.9 47.5 %reduce-scatter.61.cloned.1.call-done = bf16[192,3072]{1,0:T(8,128)(2,1)} async-done(((bf16[768,3072]{1,0:T(8,128)(2,1)}), bf16[192,3072]{1,0:T(8,128)(2,1)}) %reduce-scatter.61.cloned.1.call-update) | async-done | bytes 1179664 | tf_op jit(solution)/shard_map/reduce_scatter | solution.py:518
  662.4 50.3 %reduce-scatter.65.cloned.1.call-done = bf16[768,768]{1,0:T(8,128)(2,1)} async-done(((bf16[3072,768]{1,0:T(8,128)(2,1)}), bf16[768,768]{1,0:T(8,128)(2,1)}) %reduce-scatter.65.cloned.1.call-update) | async-done | bytes 1179664 | tf_op jit(solution)/shard_map/reduce_scatter | solution.py:524
  712.8 50.5 %reduce-scatter.93.cloned.1.call-done = bf16[192,3072]{1,0:T(8,128)(2,1)} async-done(((bf16[768,3072]{1,0:T(8,128)(2,1)}), bf16[192,3072]{1,0:T(8,128)(2,1)}) %reduce-scatter.93.cloned.1.call-update) | async-done | bytes 1179664
  767.6 56.0 %reduce-scatter.51.cloned.1.call-done = bf16[3,256,1024]{1,2,0:T(8,128)(2,1)} async-done(((bf16[3,1024,1024]{1,2,0:T(8,128)(2,1)}), bf16[3,256,1024]{1,2,0:T(8,128)(2,1)}) %reduce-scatter.51.cloned.1.call-update) | async-done | bytes 1572880 | tf_op jit(solution)/shard_map/reduce_scatter | solution.py:628
  828.1 55.8 %reduce-scatter.83.cloned.1.call-done = bf16[3,256,1024]{2,1,0:T(8,128)(2,1)} async-done(((bf16[3,1024,1024]{2,1,0:T(8,128)(2,1)}), bf16[3,256,1024]{2,1,0:T(8,128)(2,1)}) %reduce-scatter.83.cloned.1.call-update) | async-done | bytes 1572880 | tf_op jit(solution)/shard_map/reduce_scatter | solution.py:490
  907.5 64.9 %reduce-scatter.105.cloned.1.call-done = bf16[32,3]{1,0:T(8,128)(2,1)} async-done(((bf16[256,3]{1,0:T(8,128)(2,1)}), bf16[32,3]{1,0:T(8,128)(2,1)}) %reduce-scatter.105.cloned.1.call-update) | async-done | bytes 208
  973.7 63.5 %reduce-scatter.97.cloned.1.call-done = bf16[32,4]{1,0:T(8,128)(2,1)} async-done(((bf16[256,4]{1,0:T(8,128)(2,1)}), bf16[32,4]{1,0:T(8,128)(2,1)}) %reduce-scatter.97.cloned.1.call-update) | async-done | bytes 272
  1084.3 41.1 %reduce-scatter.109.cloned.1.call-done = bf16[32,8]{1,0:T(8,128)(2,1)} async-done(((bf16[256,8]{1,0:T(8,128)(2,1)}), bf16[32,8]{1,0:T(8,128)(2,1)}) %reduce-scatter.109.cloned.1.call-update) | async-done | bytes 528
  1126.8 60.6 %reduce-scatter.81.cloned.1.call-done = bf16[24,768]{1,0:T(8,128)(2,1)} async-done(((bf16[192,768]{1,0:T(8,128)(2,1)}), bf16[24,768]{1,0:T(8,128)(2,1)}) %reduce-scatter.81.cloned.1.call-update) | async-done | bytes 36880 | tf_op jit(solution)/shard_map/reduce_scatter | solution.py:501
  1188.7 63.1 %reduce-scatter.55.cloned.1.call-done = bf16[32,768]{1,0:T(8,128)(2,1)} async-done(((bf16[256,768]{1,0:T(8,128)(2,1)}), bf16[32,768]{1,0:T(8,128)(2,1)}) %reduce-scatter.55.cloned.1.call-update) | async-done | bytes 49168 | tf_op jit(solution)/shard_map/reduce_scatter | solution.py:663
  1253.3 63.6 %reduce-scatter.71.cloned.1.call-done = bf16[32,1024]{1,0:T(8,128)(2,1)} async-done(((bf16[256,1024]{1,0:T(8,128)(2,1)}), bf16[32,1024]{1,0:T(8,128)(2,1)}) %reduce-scatter.71.cloned.1.call-update) | async-done | bytes 65552 | tf_op jit(solution)/shard_map/reduce_scatter | solution.py:547
  1318.4 63.3 %reduce-scatter.75.cloned.1.call-done = bf16[32,1024]{1,0:T(8,128)(2,1)} async-done(((bf16[256,1024]{1,0:T(8,128)(2,1)}), bf16[32,1024]{1,0:T(8,128)(2,1)}) %reduce-scatter.75.cloned.1.call-update) | async-done | bytes 65552 | tf_op jit(solution)/shard_map/reduce_scatter | solution.py:553
  1383.2 63.5 %reduce-scatter.89.cloned.1.call-done = bf16[32,1024]{1,0:T(8,128)(2,1)} async-done(((bf16[256,1024]{1,0:T(8,128)(2,1)}), bf16[32,1024]{1,0:T(8,128)(2,1)}) %reduce-scatter.89.cloned.1.call-update) | async-done | bytes 65552 | tf_op jit(solution)/shard_map/reduce_scatter | solution.py:507
  1448.3 63.4 %reduce-scatter.59.cloned.1.call-done = bf16[32,1024]{1,0:T(8,128)(2,1)} async-done(((bf16[256,1024]{1,0:T(8,128)(2,1)}), bf16[32,1024]{1,0:T(8,128)(2,1)}) %reduce-scatter.59.cloned.1.call-update) | async-done | bytes 65552 | tf_op jit(solution)/shard_map/reduce_scatter | solution.py:666
  1513.2 62.6 %reduce-scatter.99.cloned.1.call-done = bf16[24,2304]{1,0:T(8,128)(2,1)} async-done(((bf16[192,2304]{1,0:T(8,128)(2,1)}), bf16[24,2304]{1,0:T(8,128)(2,1)}) %reduce-scatter.99.cloned.1.call-update) | async-done | bytes 110608
  1577.5 65.4 %reduce-scatter.63.cloned.1.call-done = bf16[24,3072]{1,0:T(8,128)(2,1)} async-done(((bf16[192,3072]{1,0:T(8,128)(2,1)}), bf16[24,3072]{1,0:T(8,128)(2,1)}) %reduce-scatter.63.cloned.1.call-update) | async-done | bytes 147472 | tf_op jit(solution)/shard_map/reduce_scatter | solution.py:538
  1644.5 65.5 %reduce-scatter.67.cloned.1.call-done = bf16[96,768]{1,0:T(8,128)(2,1)} async-done(((bf16[768,768]{1,0:T(8,128)(2,1)}), bf16[96,768]{1,0:T(8,128)(2,1)}) %reduce-scatter.67.cloned.1.call-update) | async-done | bytes 147472 | tf_op jit(solution)/shard_map/reduce_scatter | solution.py:544
  1711.7 143.8 %all-reduce.14.cloned.1.call-done = (bf16[3,192,1024]{2,0,1:T(4,128)(2,1)}, bf16[3,256,1024]{2,0,1:T(4,128)(2,1)}) async-done(((bf16[3,192,1024]{2,0,1:T(4,128)(2,1)}, bf16[3,256,1024]{2,0,1:T(4,128)(2,1)}), (bf16[3,192,1024]{2,0,1:T(4,128)(2,1)}, bf16[3,256,1024]{2,0,1:T(4,128)(2,1)})) %all-reduce.14.cloned.1.call-update) | async-done | bytes 2752528
  1859.3 64.6 %reduce-scatter.85.cloned.1.call-done = bf16[3,32,1024]{2,1,0:T(8,128)(2,1)} async-done(((bf16[3,256,1024]{2,1,0:T(8,128)(2,1)}), bf16[3,32,1024]{2,1,0:T(8,128)(2,1)}) %reduce-scatter.85.cloned.1.call-update) | async-done | bytes 196624 | tf_op jit(solution)/shard_map/reduce_scatter | solution.py:504
  (759 shorter events, 364.1 us)
Async XLA Ops:
  7.2 391.0 %reduce-scatter.103.cloned.1.call-start = ((), (), s32[]{:S(2)}) async-start(), calls=%async_computation.56 | async-start | bytes 327680
  341.8 227.3 %reduce-scatter.57.cloned.1.call-start = ((), (), s32[]{:S(2)}) async-start(), calls=%async_computation.33 | async-start | bytes 2621440 | tf_op jit(solution)/shard_map/reduce_scatter | solution.py:637
  344.0 267.8 %reduce-scatter.77.cloned.1.call-start = ((), (), s32[]{:S(2)}) async-start(), calls=%async_computation.43 | async-start | bytes 4423680 | tf_op jit(solution)/shard_map/reduce_scatter | solution.py:484
  349.6 312.8 %reduce-scatter.61.cloned.1.call-start = ((), (), s32[]{:S(2)}) async-start(), calls=%async_computation.35 | async-start | bytes 5898240 | tf_op jit(solution)/shard_map/reduce_scatter | solution.py:518
  354.3 358.4 %reduce-scatter.65.cloned.1.call-start = ((), (), s32[]{:S(2)}) async-start(), calls=%async_computation.37 | async-start | bytes 5898240 | tf_op jit(solution)/shard_map/reduce_scatter | solution.py:524
  358.9 404.4 %reduce-scatter.93.cloned.1.call-start = ((), (), s32[]{:S(2)}) async-start(), calls=%async_computation.51 | async-start | bytes 5898240
  383.4 440.1 %reduce-scatter.51.cloned.1.call-start = ((), (), s32[]{:S(2)}) async-start(), calls=%async_computation.30 | async-start | bytes 7864320 | tf_op jit(solution)/shard_map/reduce_scatter | solution.py:628
  390.2 493.7 %reduce-scatter.83.cloned.1.call-start = ((), (), s32[]{:S(2)}) async-start(), calls=%async_computation.46 | async-start | bytes 7864320 | tf_op jit(solution)/shard_map/reduce_scatter | solution.py:490
  396.7 509.9 %reduce-scatter.101.cloned.1.call-start = ((), (), s32[]{:S(2)}) async-start(), calls=%async_computation.55 | async-start | bytes 245760
  398.2 574.2 %reduce-scatter.105.cloned.1.call-start = ((), (), s32[]{:S(2)}) async-start(), calls=%async_computation.57 | async-start | bytes 73728
  398.8 638.4 %reduce-scatter.97.cloned.1.call-start = ((), (), s32[]{:S(2)}) async-start(), calls=%async_computation.53 | async-start | bytes 73728
  399.3 659.7 %reduce-scatter.107.cloned.1.call-start = ((), (), s32[]{:S(2)}) async-start(), calls=%async_computation.58 | async-start | bytes 245760
  400.9 724.5 %reduce-scatter.109.cloned.1.call-start = ((), (), s32[]{:S(2)}) async-start(), calls=%async_computation.59 | async-start | bytes 73728
  402.4 784.9 %reduce-scatter.81.cloned.1.call-start = ((), (), s32[]{:S(2)}) async-start(), calls=%async_computation.45 | async-start | bytes 331776 | tf_op jit(solution)/shard_map/reduce_scatter | solution.py:501
  403.9 847.9 %reduce-scatter.55.cloned.1.call-start = ((), (), s32[]{:S(2)}) async-start(), calls=%async_computation.32 | async-start | bytes 442368 | tf_op jit(solution)/shard_map/reduce_scatter | solution.py:663
  434.4 882.6 %reduce-scatter.71.cloned.1.call-start = ((), (), s32[]{:S(2)}) async-start(), calls=%async_computation.40 | async-start | bytes 589824 | tf_op jit(solution)/shard_map/reduce_scatter | solution.py:547
  467.9 913.8 %reduce-scatter.75.cloned.1.call-start = ((), (), s32[]{:S(2)}) async-start(), calls=%async_computation.42 | async-start | bytes 589824 | tf_op jit(solution)/shard_map/reduce_scatter | solution.py:553
  501.7 945.1 %reduce-scatter.89.cloned.1.call-start = ((), (), s32[]{:S(2)}) async-start(), calls=%async_computation.49 | async-start | bytes 589824 | tf_op jit(solution)/shard_map/reduce_scatter | solution.py:507
  535.4 976.3 %reduce-scatter.59.cloned.1.call-start = ((), (), s32[]{:S(2)}) async-start(), calls=%async_computation.34 | async-start | bytes 589824 | tf_op jit(solution)/shard_map/reduce_scatter | solution.py:666
  569.1 1006.7 %reduce-scatter.99.cloned.1.call-start = ((), (), s32[]{:S(2)}) async-start(), calls=%async_computation.54 | async-start | bytes 995328
  614.8 1028.0 %reduce-scatter.63.cloned.1.call-start = ((), (), s32[]{:S(2)}) async-start(), calls=%async_computation.36 | async-start | bytes 1327104 | tf_op jit(solution)/shard_map/reduce_scatter | solution.py:538
  662.4 1047.7 %reduce-scatter.67.cloned.1.call-start = ((), (), s32[]{:S(2)}) async-start(), calls=%async_computation.38 | async-start | bytes 1327104 | tf_op jit(solution)/shard_map/reduce_scatter | solution.py:544
  712.8 1142.7 %all-reduce.14.cloned.1.call-start = ((), (), s32[]{:S(2)}) async-start(), calls=%async_computation.60 | async-start | bytes 7340032
  828.1 1095.9 %reduce-scatter.85.cloned.1.call-start = ((), (), s32[]{:S(2)}) async-start(), calls=%async_computation.47 | async-start | bytes 1769472 | tf_op jit(solution)/shard_map/reduce_scatter | solution.py:504
  (189 other events, 1757.8 us)
Sparse Core Ops, SparseCore 0:
  436.7 31.1 reduce-scatter.68
  470.4 31.1 reduce-scatter.72
  504.2 31.1 reduce-scatter.86
  537.9 31.1 reduce-scatter.56
  571.5 40.2 reduce-scatter.76
  614.3 47.9 reduce-scatter.60
  664.7 47.9 reduce-scatter.64
  715.3 47.9 reduce-scatter.92
  765.7 57.8 reduce-scatter.50
  825.9 57.9 reduce-scatter.82
  909.9 62.4 reduce-scatter.104
  975.6 61.5 reduce-scatter.96
  1062.9 62.4 reduce-scatter.108
  1128.7 58.5 reduce-scatter.80
  1190.6 61.1 reduce-scatter.54
  1255.2 61.6 reduce-scatter.70
  1320.1 61.5 reduce-scatter.74
  1385.1 61.6 reduce-scatter.88
  1450.0 61.6 reduce-scatter.58
  1514.9 60.8 reduce-scatter.98
  1579.2 63.6 reduce-scatter.62
  1646.3 63.7 reduce-scatter.66
  1713.6 141.7 all-reduce.13
  1858.9 64.9 reduce-scatter.84
  (7 shorter events, 165.2 us)

commit v2 on v1

--- a/solution.py
+++ b/solution.py
@@ -155,6 +155,306 @@
     return [o.reshape(-1, o.shape[-1]) for o in outs]
 
 
+FIRST = ((1, 0, 2), (0, 1, 2))
+TILE = 256
+
+
+def block_axis(dim):
+    return (0, 3, 2)[dim]
+
+
+def arrange(sizes, order, values, rows):
+    X, Y, Z = sizes
+    count, width = values.shape
+    depth = width // (2 * X * Y * Z)
+    a = jnp.pad(values, ((0, rows - count), (0, 0))).T.reshape(X, 2, Z, Y, depth, rows)
+    first, second, third = (block_axis(d) for d in order)
+    a = a.transpose(1, first, second, third, 4, 5)
+    return a.reshape(2, sizes[order[0]], sizes[order[1]], sizes[order[2]] * depth, rows)
+
+
+def scatter_kernel(sizes, jobs, n_act, *refs):
+    n_grad = len(jobs)
+    n_out = max(j[2] for j in jobs) + 1
+    acts, refs = refs[:n_act], refs[n_act:]
+    grads, refs = refs[:n_grad], refs[n_grad:]
+    vec, refs = refs[0], refs[1:]
+    outs, refs = refs[:n_out], refs[n_out:]
+    vec_out, refs = refs[0], refs[1:]
+    acts2, refs = refs[:n_act], refs[n_act:]
+    grads2, refs = refs[:n_grad], refs[n_grad:]
+    vec2, refs = refs[0], refs[1:]
+    total = n_grad + 1
+    sends = [refs[3 * m:3 * m + 3] for m in range(total)]
+    refs = refs[3 * total:]
+    comes = [refs[3 * m:3 * m + 3] for m in range(total)]
+    refs = refs[3 * total:]
+    keeps = {k.shape[1]: k for k in refs[:-4]}
+    send, recv, swap_send, swap_recv = refs[-4:]
+    place, core = place_of(sizes)
+    base = slot_base(sizes)
+    greet(sizes, place, core)
+    started = []
+    swaps = {}
+
+    def swap(name, source, target):
+        at = len(swaps)
+        copy = pltpu.make_async_remote_copy(
+            source, target, swap_send.at[at], swap_recv.at[at],
+            device_id=device_of(sizes, place, 1 - core), device_id_type=MESH,
+        )
+        copy.start()
+        swaps[name] = copy
+
+    swap("vec", vec.at[1 - core], vec2)
+    for m, job in enumerate(jobs):
+        if ("a", job[0]) not in swaps:
+            swap(("a", job[0]), acts[job[0]].at[1 - core], acts2[job[0]])
+        swap(("g", m), grads[m], grads2[m])
+    settled = set()
+
+    def need(name):
+        if name not in settled:
+            settled.add(name)
+            swaps[name].wait_recv()
+
+    pending = []
+    arrive = {}
+
+    def flush(ready):
+        for copy in ready:
+            copy.start()
+            started.append(copy)
+            pending.remove(copy)
+
+    def queue(m, phase, dim):
+        waits = []
+        for step in range(1, sizes[dim]):
+            slot = base[dim] + step - 1
+            copy = pltpu.make_async_remote_copy(
+                sends[m][phase].at[step - 1], comes[m][phase].at[step - 1], send.at[m, slot], recv.at[m, slot],
+                device_id=device_of(sizes, shifted(sizes, place, dim, step), core), device_id_type=MESH,
+            )
+            waits.append(copy)
+        arrive[m, phase] = waits
+        return waits
+
+    def settle(m, phase):
+        for copy in arrive[m, phase]:
+            copy.wait_recv()
+
+    def product(m, first, second, columns):
+        act, act2, grad, grad2 = acts[jobs[m][0]], acts2[jobs[m][0]], grads[m], grads2[m]
+        return jnp.dot(
+            act[core, first, second], grad[:, columns], preferred_element_type=jnp.float32
+        ) + jnp.dot(act2[first, second], grad2[:, columns], preferred_element_type=jnp.float32)
+
+    def over_columns(width, body):
+        @pl.loop(0, width // TILE)
+        def _(i):
+            body(pl.ds(pl.multiple_of(i * TILE, TILE), TILE))
+
+    def work(m, phase):
+        ready = list(pending)
+        compute(m, phase)
+        flush(ready)
+        if phase < 3:
+            pending.extend(queue(m, phase, jobs[m][4][phase]))
+
+    def compute(m, phase):
+        _, _, out, index, order, depth, width = jobs[m]
+        d0, d1, d2 = order
+        part = sizes[d2] * depth
+        if phase == 0:
+            need(("a", jobs[m][0]))
+            need(("g", m))
+            for step in range(1, sizes[d0]):
+                there = lax.rem(place[d0] + step, sizes[d0])
+                for second in range(sizes[d1]):
+                    def body(columns, there=there, second=second, step=step):
+                        value = product(m, there, second, columns)
+                        sends[m][0][step - 1, second * part:(second + 1) * part, columns] = value.astype(jnp.bfloat16)
+                    over_columns(width, body)
+        elif phase == 1:
+            settle(m, 0)
+            for step in range(1, sizes[d1]):
+                there = lax.rem(place[d1] + step, sizes[d1])
+                rows = pl.ds(pl.multiple_of(there * part, 16), part)
+                def body(columns, there=there, rows=rows, step=step):
+                    value = product(m, place[d0], there, columns)
+                    for other in range(sizes[d0] - 1):
+                        value += comes[m][0][other, rows, columns].astype(jnp.float32)
+                    sends[m][1][step - 1, :, columns] = value.astype(jnp.bfloat16)
+                over_columns(width, body)
+        elif phase == 2:
+            settle(m, 1)
+            rows = pl.ds(pl.multiple_of(place[d1] * part, 16), part)
+            keep = keeps[width]
+            def body(columns):
+                value = product(m, place[d0], place[d1], columns)
+                for other in range(sizes[d0] - 1):
+                    value += comes[m][0][other, rows, columns].astype(jnp.float32)
+                for other in range(sizes[d1] - 1):
+                    value += comes[m][1][other, :, columns].astype(jnp.float32)
+                keep[:part, columns] = value
+                for step in range(1, sizes[d2]):
+                    there = pl.ds(pl.multiple_of(lax.rem(place[d2] + step, sizes[d2]) * depth, 8), depth)
+                    sends[m][2][step - 1, :, columns] = keep[there, columns].astype(jnp.bfloat16)
+                here = pl.ds(pl.multiple_of(place[d2] * depth, 8), depth)
+                target = outs[out] if index is None else outs[out].at[index]
+                target[:, columns] = keep[here, columns]
+            over_columns(width, body)
+        else:
+            settle(m, 2)
+            target = outs[out] if index is None else outs[out].at[index]
+            def body(columns):
+                value = target[:, columns]
+                for other in range(sizes[d2] - 1):
+                    value += comes[m][2][other, :, columns].astype(jnp.float32)
+                target[:, columns] = value
+            over_columns(width, body)
+
+    last = n_grad
+
+    def vec_work(phase):
+        d0, d1, d2 = FIRST[0]
+        if phase == 0:
+            need("vec")
+            vec2[...] = vec2[...] + vec[core]
+            for step in range(1, sizes[d0]):
+                sends[last][0][step - 1] = vec2[lax.rem(place[d0] + step, sizes[d0])]
+        elif phase == 1:
+            settle(last, 0)
+            value = vec2[place[d0]]
+            for other in range(sizes[d0] - 1):
+                value += comes[last][0][other]
+            vec2[place[d0]] = value
+            for step in range(1, sizes[d1]):
+                sends[last][1][step - 1] = vec2[place[d0], lax.rem(place[d1] + step, sizes[d1])]
+        elif phase == 2:
+            settle(last, 1)
+            value = vec2[place[d0], place[d1]]
+            for other in range(sizes[d1] - 1):
+                value += comes[last][1][other]
+            vec2[place[d0], place[d1]] = value
+            for step in range(1, sizes[d2]):
+                sends[last][2][step - 1] = vec2[place[d0], place[d1], lax.rem(place[d2] + step, sizes[d2])]
+        else:
+            settle(last, 2)
+            value = vec2[place[d0], place[d1], place[d2]]
+            for other in range(sizes[d2] - 1):
+                value += comes[last][2][other]
+            vec_out[...] = value
+        if phase < 3:
+            pending.extend(queue(last, phase, FIRST[0][phase]))
+
+    lag = 2
+    for s in range(n_grad + 3 * lag):
+        for phase in (3, 2, 1, 0):
+            m = s - lag * phase
+            if 0 <= m < n_grad:
+                work(m, phase)
+        if s < 4 * lag and s % lag == 0:
+            vec_work(s // lag)
+    flush(list(pending))
+    for copy in started:
+        copy.wait_send()
+    for copy in swaps.values():
+        copy.wait_send()
+
+
+def scatter(sizes, acts, jobs, grads, vec, collective_id=1):
+    n_act, total = len(acts), len(jobs) + 1
+    X, Y, Z = sizes
+    vmem = pl.BlockSpec(memory_space=pltpu.VMEM)
+    shapes = {}
+    for _, _, out, index, _, depth, width in jobs:
+        shapes[out] = (depth, width) if index is None else (3, depth, width)
+    outs = [jax.ShapeDtypeStruct(shapes[k], jnp.float32) for k in sorted(shapes)]
+    outs.append(jax.ShapeDtypeStruct(vec.shape[4:], jnp.float32))
+    scratch = [pltpu.VMEM(a.shape[1:], a.dtype) for a in acts]
+    scratch += [pltpu.VMEM(g.shape, g.dtype) for g in grads]
+    scratch.append(pltpu.VMEM(vec.shape[1:], jnp.float32))
+    stages, keeps = [], {}
+    for _, _, _, _, order, depth, width in jobs:
+        a, b, c = (sizes[d] for d in order)
+        stages += [
+            pltpu.VMEM((a - 1, b * c * depth, width), jnp.bfloat16),
+            pltpu.VMEM((b - 1, c * depth, width), jnp.bfloat16),
+            pltpu.VMEM((c - 1, depth, width), jnp.bfloat16),
+        ]
+        keeps[width] = max(keeps.get(width, 0), c * depth)
+    a, b, c = (sizes[d] for d in FIRST[0])
+    tail = vec.shape[4:]
+    stages += [
+        pltpu.VMEM((a - 1, b, c, *tail), jnp.float32),
+        pltpu.VMEM((b - 1, c, *tail), jnp.float32),
+        pltpu.VMEM((c - 1, *tail), jnp.float32),
+    ]
+    scratch += stages + stages
+    scratch += [pltpu.VMEM((rows, width), jnp.float32) for width, rows in sorted(keeps.items())]
+    slots = sum(sizes) - 3
+    swaps = 1 + len(grads) + len({j[0] for j in jobs})
+    scratch += [pltpu.SemaphoreType.DMA((total, slots))] * 2 + [pltpu.SemaphoreType.DMA((swaps,))] * 2
+    return pl.pallas_call(
+        functools.partial(scatter_kernel, sizes, jobs, n_act),
+        out_shape=outs,
+        in_specs=[vmem] * (n_act + len(grads) + 1),
+        out_specs=[vmem] * len(outs),
+        scratch_shapes=scratch,
+        compiler_params=pltpu.CompilerParams(
+            collective_id=collective_id, has_side_effects=True, vmem_limit_bytes=66000000
+        ),
+    )(*acts, *grads, vec)
+
+
+def padded(count):
+    return -(-count // 16) * 16
+
+
+def reduce_all(sizes, work, small_grads):
+    X, Y, Z = sizes
+    devices = 2 * X * Y * Z
+    sums = [jnp.concatenate([jnp.atleast_2d(a).reshape(-1, devices, a.shape[-1] // devices).transpose(1, 0, 2).reshape(devices, -1) for a in small_grads], 1)]
+    vec = jnp.pad(sums[0], ((0, 0), (0, 1024 - sums[0].shape[1])))
+    depths = [a.shape[1] // devices for a, _, _ in work]
+    if any(d % 8 or d * Z % 16 for d in depths):
+        axes = ("gx", "gy")
+        results = []
+        for a, gs, _ in work:
+            for_each = [
+                lax.psum_scatter(
+                    lax.dot_general(a, g, (((0,), (0,)), ((), ())), preferred_element_type=jnp.float32).astype(jnp.bfloat16),
+                    axes, scatter_dimension=0, tiled=True,
+                ).astype(jnp.float32)
+                for g in gs
+            ]
+            results.append(for_each[0] if len(gs) == 1 else jnp.stack(for_each))
+        vec_sum = lax.psum_scatter(vec, axes, scatter_dimension=0, tiled=True).reshape(-1)
+    else:
+        acts, jobs, grads = [], [], []
+        for position, (a, gs, kind) in enumerate(work):
+            rows = padded(a.shape[0])
+            acts.append(arrange(sizes, FIRST[kind], a, rows))
+            for index, g in enumerate(gs):
+                jobs.append((
+                    position, len(grads), position, index if len(gs) > 1 else None,
+                    FIRST[kind], a.shape[1] // devices, g.shape[1],
+                ))
+                grads.append(jnp.pad(g, ((0, rows - g.shape[0]), (0, 0))))
+        first, second, third = (block_axis(d) for d in FIRST[0])
+        vec = vec.reshape(X, 2, Z, Y, 8, 128).transpose(1, first, second, third, 4, 5)
+        results = scatter(sizes, acts, tuple(jobs), grads, vec)
+        results, vec_sum = results[:-1], results[-1].reshape(-1)
+    smalls, at = [], 0
+    for a in small_grads:
+        count = a.size // devices
+        part = vec_sum[at:at + count]
+        smalls.append(part if a.ndim == 1 else part.reshape(a.shape[0], -1))
+        at += count
+    return results, smalls
+
+
 HT = 12
 HV = 8
 CHN = 8
@@ -180,14 +480,11 @@
 
 
 def linear_back(inputs, weight, grad_low):
-    weight_grad = lax.dot_general(
-        inputs, grad_low, (((0,), (0,)), ((), ())), preferred_element_type=jnp.float32
-    )
     input_grad = lax.dot_general(
         grad_low, weight, (((1,), (1,)), ((), ())), preferred_element_type=jnp.float32
     )
     bias_grad = jnp.sum(grad_low.astype(jnp.float32), 0)
-    return (weight_grad, bias_grad, input_grad)
+    return (grad_low, bias_grad, input_grad)
 
 
 def split_heads(values, pair_count, head_count):
@@ -257,7 +554,7 @@
 
 def projections_back(inputs, weights, grads):
     outcomes = [linear_back(inputs, weights[position], grads[position]) for position in range(3)]
-    stacked = jnp.stack([outcome[0] for outcome in outcomes])
+    stacked = tuple(grads)
     input_grad = outcomes[0][2] + outcomes[1][2] + outcomes[2][2]
     return (stacked, outcomes[0][1], outcomes[2][1], input_grad)
 
@@ -480,79 +777,11 @@
         pair_count,
         image_cot.reshape(pair_count * region_count, image_width).astype(jnp.float32),
     )
-    self_partial = (
-        lax.psum_scatter(
-            text_self_grads[0].astype(jnp.bfloat16), "gx", scatter_dimension=1, tiled=True
-        ).astype(jnp.float32),
-        lax.psum_scatter(
-            text_self_grads[1].astype(jnp.bfloat16), "gx", scatter_dimension=0, tiled=True
-        ).astype(jnp.float32),
-        lax.psum_scatter(
-            image_self_grads[0].astype(jnp.bfloat16), "gx", scatter_dimension=1, tiled=True
-        ).astype(jnp.float32),
-        lax.psum_scatter(
-            image_self_grads[1].astype(jnp.bfloat16), "gx", scatter_dimension=0, tiled=True
-        ).astype(jnp.float32),
-    )
-    self_sums = (
-        lax.psum_scatter(
-            self_partial[0].astype(jnp.bfloat16), "gy", scatter_dimension=1, tiled=True
-        ).astype(jnp.float32),
-        lax.psum_scatter(
-            self_partial[1].astype(jnp.bfloat16), "gy", scatter_dimension=0, tiled=True
-        ).astype(jnp.float32),
-        lax.psum_scatter(
-            self_partial[2].astype(jnp.bfloat16), "gy", scatter_dimension=1, tiled=True
-        ).astype(jnp.float32),
-        lax.psum_scatter(
-            self_partial[3].astype(jnp.bfloat16), "gy", scatter_dimension=0, tiled=True
-        ).astype(jnp.float32),
-    )
     text_feed_grads = feed_back(
         text_feed_kept, feed_full[0], feed_full[2], text_self_grads[7]
     )
     image_feed_grads = feed_back(
         image_feed_kept, feed_full[3], feed_full[5], image_self_grads[7]
-    )
-    feed_partial = (
-        lax.psum_scatter(
-            text_feed_grads[0].astype(jnp.bfloat16), "gx", scatter_dimension=0, tiled=True
-        ).astype(jnp.float32),
-        lax.psum_scatter(
-            text_feed_grads[1].astype(jnp.bfloat16), "gx", scatter_dimension=0, tiled=True
-        ).astype(jnp.float32),
-        lax.psum_scatter(
-            text_feed_grads[2].astype(jnp.bfloat16), "gx", scatter_dimension=0, tiled=True
-        ).astype(jnp.float32),
-        lax.psum_scatter(
-            image_feed_grads[0].astype(jnp.bfloat16), "gx", scatter_dimension=0, tiled=True
-        ).astype(jnp.float32),
-        lax.psum_scatter(
-            image_feed_grads[1].astype(jnp.bfloat16), "gx", scatter_dimension=0, tiled=True
-        ).astype(jnp.float32),
-        lax.psum_scatter(
-            image_feed_grads[2].astype(jnp.bfloat16), "gx", scatter_dimension=0, tiled=True
-        ).astype(jnp.float32),
-    )
-    feed_sums = (
-        lax.psum_scatter(
-            feed_partial[0].astype(jnp.bfloat16), "gy", scatter_dimension=0, tiled=True
-        ).astype(jnp.float32),
-        lax.psum_scatter(
-            feed_partial[1].astype(jnp.bfloat16), "gy", scatter_dimension=0, tiled=True
-        ).astype(jnp.float32),
-        lax.psum_scatter(
-            feed_partial[2].astype(jnp.bfloat16), "gy", scatter_dimension=0, tiled=True
-        ).astype(jnp.float32),
-        lax.psum_scatter(
-            feed_partial[3].astype(jnp.bfloat16), "gy", scatter_dimension=0, tiled=True
-        ).astype(jnp.float32),
-        lax.psum_scatter(
-            feed_partial[4].astype(jnp.bfloat16), "gy", scatter_dimension=0, tiled=True
-        ).astype(jnp.float32),
-        lax.psum_scatter(
-            feed_partial[5].astype(jnp.bfloat16), "gy", scatter_dimension=0, tiled=True
-        ).astype(jnp.float32),
     )
     text_pre_grad, text_first_gain_grad, text_first_shift_grad = text_norm_back(text_feed_grads[6])
     image_pre_grad, image_first_gain_grad, image_first_shift_grad = image_norm_back(
@@ -621,63 +850,27 @@
             image_self_grads[6],
         ]
     )
-    cross_partial = (
-        lax.psum_scatter(
-            text_proj_grad.astype(jnp.bfloat16), "gx", scatter_dimension=1, tiled=True
-        ).astype(jnp.float32),
-        lax.psum_scatter(
-            image_proj_grad.astype(jnp.bfloat16), "gx", scatter_dimension=1, tiled=True
-        ).astype(jnp.float32),
-        lax.psum_scatter(
-            cross_bias_grad.astype(jnp.bfloat16), "gx", scatter_dimension=1, tiled=True
-        ).astype(jnp.float32),
-        lax.psum_scatter(
-            text_out_grad.astype(jnp.bfloat16), "gx", scatter_dimension=0, tiled=True
-        ).astype(jnp.float32),
-        lax.psum_scatter(
-            image_out_grad.astype(jnp.bfloat16), "gx", scatter_dimension=0, tiled=True
-        ).astype(jnp.float32),
-        lax.psum_scatter(
-            text_gains_grad.astype(jnp.bfloat16), "gx", scatter_dimension=1, tiled=True
-        ).astype(jnp.float32),
-        lax.psum_scatter(
-            image_gains_grad.astype(jnp.bfloat16), "gx", scatter_dimension=1, tiled=True
-        ).astype(jnp.float32),
-        lax.psum_scatter(
-            text_vectors_grad.astype(jnp.bfloat16), "gx", scatter_dimension=1, tiled=True
-        ).astype(jnp.float32),
-        lax.psum_scatter(
-            image_vectors_grad.astype(jnp.bfloat16), "gx", scatter_dimension=1, tiled=True
-        ).astype(jnp.float32),
-    )
-    cross_sums = (
-        lax.psum_scatter(
-            cross_partial[0].astype(jnp.bfloat16), "gy", scatter_dimension=1, tiled=True
-        ).astype(jnp.float32),
-        lax.psum_scatter(
-            cross_partial[1].astype(jnp.bfloat16), "gy", scatter_dimension=1, tiled=True
-        ).astype(jnp.float32),
-        lax.psum_scatter(
-            cross_partial[2].astype(jnp.bfloat16), "gy", scatter_dimension=1, tiled=True
-        ).astype(jnp.float32),
-        lax.psum_scatter(
-            cross_partial[3].astype(jnp.bfloat16), "gy", scatter_dimension=0, tiled=True
-        ).astype(jnp.float32),
-        lax.psum_scatter(
-            cross_partial[4].astype(jnp.bfloat16), "gy", scatter_dimension=0, tiled=True
-        ).astype(jnp.float32),
-        lax.psum_scatter(
-            cross_partial[5].astype(jnp.bfloat16), "gy", scatter_dimension=1, tiled=True
-        ).astype(jnp.float32),
-        lax.psum_scatter(
-            cross_partial[6].astype(jnp.bfloat16), "gy", scatter_dimension=1, tiled=True
-        ).astype(jnp.float32),
-        lax.psum_scatter(
-            cross_partial[7].astype(jnp.bfloat16), "gy", scatter_dimension=1, tiled=True
-        ).astype(jnp.float32),
-        lax.psum_scatter(
-            cross_partial[8].astype(jnp.bfloat16), "gy", scatter_dimension=1, tiled=True
-        ).astype(jnp.float32),
+    work = (
+        (text_self_kept[4], (text_self_grads[1],), 1),
+        (image_self_kept[4], (image_self_grads[1],), 0),
+        (text_self_kept[0], text_self_grads[0], 0),
+        (image_self_kept[0], image_self_grads[0], 1),
+        (text_feed_kept[1], (text_feed_grads[2],), 1),
+        (image_feed_kept[1], (image_feed_grads[2],), 0),
+        (text_feed_kept[0], (text_feed_grads[0],), 0),
+        (image_feed_kept[0], (image_feed_grads[0],), 0),
+        (text_mixture, (text_out_grad,), 1),
+        (image_mixture, (image_out_grad,), 1),
+        (text_rows, text_proj_grad, 1),
+        (image_rows, image_proj_grad, 0),
+    )
+    sums, smalls = reduce_all(
+        sizes,
+        work,
+        (
+            cross_bias_grad, text_gains_grad, image_gains_grad, text_vectors_grad, image_vectors_grad,
+            text_feed_grads[1], image_feed_grads[1],
+        ),
     )
     text_in_grad = (
         (text_pre_grad + text_input_grad)
@@ -694,25 +887,25 @@
         image_out,
         text_in_grad,
         image_in_grad,
-        cross_sums[0],
-        cross_sums[1],
-        cross_sums[2],
-        cross_sums[3],
-        cross_sums[4],
-        feed_sums[0],
-        feed_sums[1],
-        feed_sums[2],
-        feed_sums[3],
-        feed_sums[4],
-        feed_sums[5],
-        self_sums[0],
-        self_sums[1],
-        self_sums[2],
-        self_sums[3],
-        cross_sums[5],
-        cross_sums[6],
-        cross_sums[7],
-        cross_sums[8],
+        sums[10],
+        sums[11],
+        smalls[0],
+        sums[8],
+        sums[9],
+        sums[6],
+        smalls[5],
+        sums[4],
+        sums[7],
+        smalls[6],
+        sums[5],
+        sums[2],
+        sums[0],
+        sums[3],
+        sums[1],
+        smalls[1],
+        smalls[2],
+        smalls[3],
+        smalls[4],
     )
 
 

time: 1940 us -> 668 us (0.34)
  waiting for transfers between devices: 1440 us -> 0 us
  Pallas kernels: 194 us -> 478 us
  other arithmetic: 50.1 us -> 16.1 us
  matrix products: 105 us -> 74.7 us
  blocking collectives: 27.8 us -> 0 us
    reduce_scatter x21 -> x0, waiting for transfers between devices: 992 us -> none  [the longest x1 65.5 us: per_device(): lax.psum_scatter(feed_partial[2].astype(jnp.bfloat16), 'gy', scatter_dime...]
    unnamed x41 -> x0, waiting for transfers between devices: 453 us -> none
    pallas_call x0 -> x1, Pallas kernels: none -> 284 us  [scatter(): pl.pallas_call(functools.partial(scatter_kernel, sizes, jobs, n_act), out...]
    unnamed x416 -> x373, local copies, waits for them, and re-layouts: 53.1 us -> 18 us
    dot_general x20 -> x0, matrix products: 29.4 us -> none  [linear_back(): lax.dot_general(inputs, grad_low, (((0,), (0,)), ((), ())), preferred_ele...]
    unnamed x2 -> x0, blocking collectives: 27.8 us -> none
    convert_element_type x19 -> x1, other arithmetic: 20.8 us -> 0.09 us  [feed_forward(): normed_low = normed.astype(jnp.bfloat16)]
  transfers between devices with their start and end apart: 31 -> 0, of which waited for: 28 -> 0; matrix products, arithmetic and copies ran while one was open for 9% -> 0% of each run, Pallas kernels for 0% -> 0%
where the time goes in v2:
time: 668 us; the launch traced here: 656 us
  Pallas kernels  478 us (72%)
  local copies, waits for them, and re-layouts  83.1 us (12%)
  matrix products  74.7 us (11%)
  other arithmetic  16.1 us (2%)
    pallas_call x1, Pallas kernels, scatter(): pl.pallas_call(functools.partial(scatter_kernel, sizes, jobs, n_act), out...  284 us
    pallas_call x1, Pallas kernels, gather(): pl.pallas_call(functools.partial(gather_kernel, sizes, pieces, ahead), ou...  194 us
    dot_general x20, matrix products, project(): return jnp.dot(inputs, weight, preferred_element_type=jnp.float32)  34.5 us
    dot_general x20, matrix products, linear_back(): lax.dot_general(grad_low, weight, (((1,), (1,)), ((), ())), preferred_ele...  30.1 us
    unnamed x373, local copies, waits for them, and re-layouts  18 us

profile of v2, /device:TPU:0, one launch (start us, length us, event | category | flops | bytes accessed | tf_op | source)
XLA Modules:
  0.0 656.3 jit_solution(1578768493498474122)
XLA Ops:
  6.5 194.3 %shard_map.416 = (bf16[2,2,4,2,8,128]{5,4,3,2,1,0:T(8,128)(2,1)}, bf16[2,2,4,2,24,1024]{5,4,3,2,1,0:T(8,128)(2,1)}, bf16[2,2,4,2,24,1024]{5,4,3,2,1,0:T(8,128)(2...) custom-call(bf16[8,128]{1,0:T(8,128)(2,1)} %pad_bitcast_fusion.7.ref, ...), custom_call_target="tpu_custom_call" | custom-call | tf_op jit(solution)/shard_map/pallas_call | solution.py:114
  202.7 2.2 fusion.26
  207.1 2.2 fusion.2
  213.1 2.8 multiply_convert_fusion.5
  217.8 2.2 fusion.28
  221.4 2.1 fusion.27
  224.6 2.2 fusion.128
  229.2 1.6 fusion.113
  230.9 2.4 convolution_convert_fusion.11
  245.2 2.2 convolution_convert_fusion.15
  250.9 1.9 fusion.120
  254.2 4.7 multiply_convert_fusion
  258.9 3.3 fusion.121
  263.4 1.6 fusion.12
  265.8 1.6 fusion.11
  268.3 1.7 fusion.123
  271.4 1.9 fusion.116
  274.6 1.7 copy.126
  284.8 5.0 convert_reduce_fusion
  289.9 2.3 multiply_reduce_fusion.2
  311.2 2.2 fusion.15
  316.2 1.7 convolution_convert_fusion.9
  345.4 283.5 %shard_map.417 = (f32[24,768]{1,0:T(8,128)}, f32[32,1024]{1,0:T(8,128)}, f32[3,24,768]{2,1,0:T(8,128)}, f32[3,32,1024]{2,1,0:T(8,128)}, f32[96,768]{1,0:T(8,128)...) custom-call(bf16[2,2,2,96,128]{4,3,2,1,0:T(8,128)(2,1)} %bitcast.552, ...), custom_call_target="tpu_custom_call" | custom-call | tf_op jit(solution)/shard_map/pallas_call | solution.py:399
  637.8 2.3 fusion.132
  (649 shorter events, 122.1 us)
Async XLA Ops:
  0.7 202.1 %copy-start.43 = (bf16[1,36,1024]{2,1,0:T(8,128)(2,1)S(1)}, bf16[1,36,1024]{2,1,0:T(8,128)(2,1)}, u32[]{:S(2)}) copy-start(bf16[1,36,1024]{2,1,0:T(8,128)(2,1)} %param.26) | copy-start | bytes 221188
  201.7 11.2 %copy-start.109 = (bf16[4,8,8,128]{3,1,2,0:T(8,128)(2,1)}, bf16[4,8,8,128]{3,1,2,0:T(8,128)(2,1)S(1)}, u32[]{:S(2)}) copy-start(bf16[4,8,8,128]{3,1,2,0:T(8,128)(2,1)S(1)} %copy.306) | copy-start | bytes 196612
  223.8 5.3 copy-start.77
  262.3 21.1 %copy-start.134 = (f32[128]{0:T(128)}, f32[128]{0:T(128)S(1)}, u32[]{:S(2)}) copy-start(f32[128]{0:T(128)S(1)} %broadcast_multiply_fusion.4) | copy-start | bytes 1540
  262.5 20.9 %copy-start.136 = (f32[128]{0:T(128)}, f32[128]{0:T(128)S(1)}, u32[]{:S(2)}) copy-start(f32[128]{0:T(128)S(1)} %fusion.101) | copy-start | bytes 1540
  283.4 6.5 slice-start
  283.7 6.1 copy-start.68
  295.5 20.7 %copy-start.5 = (bf16[2,2,4,2,32,1024]{5,4,3,2,1,0:T(8,128)(2,1)S(1)}, bf16[2,2,4,2,32,1024]{5,4,3,2,1,0:T(8,128)(2,1)}, u32[]{:S(2)}) copy-start(bf16[2,2,4,2,32,1024]{5,4,3,2,1,0:T(8,128)(2,1)} %get-tuple-element.71) | copy-start | bytes 6291460
  319.5 5.8 copy-start.29
  320.4 11.5 %copy-start.65 = (bf16[8,128,128]{2,1,0:T(8,128)(2,1)}, bf16[8,128,128]{2,1,0:T(8,128)(2,1)S(1)}, u32[]{:S(2)}) copy-start(bf16[8,128,128]{2,1,0:T(8,128)(2,1)S(1)} %get-tuple-element.211) | copy-start | bytes 786436
  323.8 5.5 copy-start.82
  323.8 6.1 copy-start.84
  323.9 6.7 %copy-start.86 = (bf16[5,8,8,128]{3,1,2,0:T(8,128)(2,1)S(1)}, bf16[5,8,8,128]{3,1,2,0:T(8,128)(2,1)}, u32[]{:S(2)}) copy-start(bf16[5,8,8,128]{3,1,2,0:T(8,128)(2,1)} %copy-done.85) | copy-start | bytes 245764
  324.5 6.7 %copy-start.80 = (bf16[36,1024]{1,0:T(8,128)(2,1)S(1)}, bf16[36,1024]{1,0:T(8,128)(2,1)}, u32[]{:S(2)}) copy-start(bf16[36,1024]{1,0:T(8,128)(2,1)} %copy-done.79) | copy-start | bytes 221188
  325.3 7.5 %copy-start.67 = (bf16[768,128]{0,1:T(8,128)(2,1)S(1)}, bf16[768,128]{0,1:T(8,128)(2,1)}, u32[]{:S(2)}) copy-start(bf16[768,128]{0,1:T(8,128)(2,1)} %get-tuple-element.158) | copy-start | bytes 589828
  326.4 7.2 %copy-start.48 = (bf16[12,64,128]{2,1,0:T(8,128)(2,1)S(1)}, bf16[12,64,128]{2,1,0:T(8,128)(2,1)}, u32[]{:S(2)}) copy-start(bf16[12,64,128]{2,1,0:T(8,128)(2,1)} %copy-done.47) | copy-start | bytes 589828
  327.3 7.1 %copy-start.52 = (bf16[12,64,128]{2,1,0:T(8,128)(2,1)S(1)}, bf16[12,64,128]{2,1,0:T(8,128)(2,1)}, u32[]{:S(2)}) copy-start(bf16[12,64,128]{2,1,0:T(8,128)(2,1)} %copy-done.51) | copy-start | bytes 589828
  328.0 7.3 %copy-start.54 = (bf16[12,64,128]{2,1,0:T(8,128)(2,1)S(1)}, bf16[12,64,128]{2,1,0:T(8,128)(2,1)}, u32[]{:S(2)}) copy-start(bf16[12,64,128]{2,1,0:T(8,128)(2,1)} %copy-done.53) | copy-start | bytes 589828
  329.3 6.8 %copy-start.78 = (bf16[5,8,8,128]{3,1,2,0:T(8,128)(2,1)S(1)}, bf16[5,8,8,128]{3,1,2,0:T(8,128)(2,1)}, u32[]{:S(2)}) copy-start(bf16[5,8,8,128]{3,1,2,0:T(8,128)(2,1)} %copy-done.77) | copy-start | bytes 245764
  345.4 292.5 %copy-start.95 = (bf16[5,8,8,128]{3,1,2,0:T(8,128)(2,1)S(1)}, bf16[5,8,8,128]{3,1,2,0:T(8,128)(2,1)}, u32[]{:S(2)}) copy-start(bf16[5,8,8,128]{3,1,2,0:T(8,128)(2,1)} %copy-done.94) | copy-start | bytes 245764
  628.9 11.3 %copy-start.2 = (bf16[2,2,4,2,32,1024]{5,4,3,2,1,0:T(8,128)(2,1)S(1)}, bf16[2,2,4,2,32,1024]{5,4,3,2,1,0:T(8,128)(2,1)}, u32[]{:S(2)}) copy-start(bf16[2,2,4,2,32,1024]{5,4,3,2,1,0:T(8,128)(2,1)} %get-tuple-element.60) | copy-start | bytes 6291460
  628.9 11.3 %copy-start.93 = (bf16[5,8,8,128]{3,1,2,0:T(8,128)(2,1)S(1)}, bf16[5,8,8,128]{3,1,2,0:T(8,128)(2,1)}, u32[]{:S(2)}) copy-start(bf16[5,8,8,128]{3,1,2,0:T(8,128)(2,1)} %copy-done.92) | copy-start | bytes 245764
  648.3 5.5 copy-start.126
  648.3 6.1 copy-start.100
  (139 other events, 334.1 us)
